TPU v7x, 256 devices: a whole 4x4x8 slice. The times are simulated.
256 devices in a mesh: leaf: 128 (over x, y, z), sub: 2 (over core).
Axes of the slice: x: 4, y: 4, z: 8, core: 2. Of those that a mesh axis runs over, the one named last changes fastest.
Arguments:
- points: float32 [2, 2097152], P(None, ('leaf', 'sub')), may hold values from 0 to 1
- right_sides: float32 [32, 2097152], P(None, ('leaf', 'sub')), may hold values from -0.6 to 0.6
- leaf_order: int32 [16384], P(('leaf', 'sub')), may hold values from 0 to 63, as said below
- leaf_basis: float32 [16384, 32, 128], P(('leaf', 'sub')), may hold values from -0.5 to 0.5
- transfer_low: float32 [4096, 32, 128], P(('leaf', 'sub')), may hold values from -0.5 to 0.5
- transfer_top: float32 [4096, 32, 32], P(('leaf', 'sub')), may hold values from -0.1875 to 0.1875
- proxy_low: float32 [4096, 2, 32], P(('leaf', 'sub')), may hold values from 0 to 1
- proxy_top: float32 [128, 2, 32], replicated, may hold values from 0 to 1
- near_lists: int32 [16384, 9], P(('leaf', 'sub')), may hold values from 0 to 16383, as said below
- far_lists: int32 [4096, 27], P(('leaf', 'sub')), may hold values from 0 to 4095, as said below
- top_lists: int32 [128, 27], P('leaf'), may hold values from 0 to 127
- subtree_map: int32 [128], replicated, may hold values from 0 to 127, each once
Outputs:
- product: float32 [32, 2097152], P(None, ('leaf', 'sub'))
Inputs may be any that keep to these rules, and one draw needn't show every extreme that they name: `leaf_order`: each device's block of 64 entries is a permutation of 0 to 63. `near_lists`: entries are global leaf numbers; leaf s lies on device s // 64, devices numbered leaf index times the size of sub plus sub index and laid out in rows of 16. Of the entries of one device's leaves exactly 256 lie on other devices, all on the devices beside it in its row or in its column (number one less or one more in the same row of 16, or 16 less or 16 more), at most 128 on any one of them, and for every device some such neighbour holds exactly 128. `far_lists`: entries are global cluster numbers; cluster s lies on device s // 16, and the sources of a device's clusters lie on that device or on the devices numbered one less or one more.
All inputs are finite; a program needn't handle non-finite values.
Results may differ from a plain program's by a relative error of at most 0.00017.
Values sent between devices are 32-bit elements; how exact they have to be, the bound alone decides.
No kernel may reach another device: no remote copies, remote signals or barrier semaphores. Data moves between devices by JAX's collectives and lax.ppermute only.
A program may use at most 128 MiB of HBM per device.

v0:
```python
import jax
import jax.numpy as jnp
import numpy as np
from jax import lax
from jax.experimental import pallas as pl
from jax.experimental.pallas import tpu as pltpu
from jax.sharding import PartitionSpec as P


LEAF = 128
RANK = 32
RHS = 32
LPD = 64
NEAR = 9
FAR = 27
LOCAL = LPD * NEAR - 256
UNROLL = 8
UP_UNROLL = 4
WINDOW = 2176
LIST = 640
AXES = ("leaf", "sub")
MIB = 1024 * 1024
RATE = float(-4.0 / np.log(2.0))
TINY = 1e-30
f32 = jnp.float32
bf16 = jnp.bfloat16
VMEM = pl.BlockSpec(memory_space=pltpu.VMEM)
SMEM = pl.BlockSpec(memory_space=pltpu.SMEM)
HBM = pl.BlockSpec(memory_space=pltpu.HBM)


def decay(delta_x, delta_y):
    square = jnp.maximum(delta_x * delta_x + delta_y * delta_y, TINY)
    return jnp.exp2((square * lax.rsqrt(square)) * RATE)


def split(x):
    high = x.astype(bf16)
    return high, (x - high.astype(f32)).astype(bf16)


def dot(a, b, contract=((1,), (0,))):
    return lax.dot_general(a, b, (contract, ((), ())), preferred_element_type=f32)


def dot3(a, b, contract=((1,), (0,))):
    a_high, a_low = split(a)
    b_high, b_low = split(b)
    return (
        dot(a_high, b_high, contract) + dot(a_high, b_low, contract) + dot(a_low, b_high, contract)
    )


def lanes(x, lane):
    index = jnp.full(x.shape, lane, jnp.int32)
    return jnp.take_along_axis(x, index, axis=1, mode="promise_in_bounds")


def fetch(pairs, semaphores):
    copies = [
        pltpu.make_async_copy(source, target, semaphores.at[number])
        for number, (source, target) in enumerate(pairs)
    ]
    for copy in copies:
        copy.start()
    return copies


def pack_kernel(order_in, points_in, values_in, out, order, points, values, semaphores):
    pairs = ((order_in, order), (points_in, points), (values_in, values))
    for copy in fetch(pairs, semaphores):
        copy.wait()
    for leaf in range(LPD):
        columns = pl.ds(pl.multiple_of(order[leaf] * LEAF, LEAF), LEAF)
        out[32 * leaf : 32 * leaf + 32, :] = values[:, columns]
        out[2048 + 2 * leaf : 2048 + 2 * leaf + 2, :] = points[:, columns]


def up_kernel(
    device,
    near_in,
    pack,
    basis_in,
    low_in,
    top_in,
    proxy_in,
    halo,
    weights_out,
    tasks,
    near,
    basis,
    low,
    top,
    proxy,
    weights,
    coef,
    semaphores,
):
    pairs = (
        (near_in, near),
        (low_in, low),
        (basis_in, basis),
        (top_in, top),
        (proxy_in, proxy),
    )
    copies = fetch(pairs, semaphores)
    base = device[0] * LPD
    row_block = lax.broadcasted_iota(jnp.int32, (128, 128), 0) // 32
    lane_block = lax.broadcasted_iota(jnp.int32, (128, 128), 1) // 32
    diagonal = row_block == lane_block
    for copy in copies[:3]:
        copy.wait()

    def sort_leaf(leaf, local):
        code = leaf * 4096 + 1024 - base
        for k in range(NEAR):
            entry = near[k, leaf]
            offset = entry - base
            home = (offset >= 0) & (offset < LPD)
            where = jnp.where(home, local, (leaf * NEAR + (k + LOCAL)) - local)
            tasks[where] = entry + code
            local = local + home.astype(jnp.int32)
        return local

    def cluster(number, local):
        transfer = low[number]
        stacked = jnp.where(diagonal, jnp.concatenate([transfer] * 4, axis=0), 0.0)
        bases = basis[pl.ds(4 * number, 4)].reshape(128, LEAF)
        product = dot3(stacked, bases)
        rows = pl.ds(pl.multiple_of(128 * number, 128), 128)
        weights[rows, :] = product
        x = pack[rows, :]
        wide_w = jnp.concatenate([product[32 * m : 32 * m + 32] for m in range(4)], axis=1)
        wide_x = jnp.concatenate([x[32 * m : 32 * m + 32] for m in range(4)], axis=1)
        coef[pl.ds(pl.multiple_of(32 * number, 32), 32), 0:32] = dot3(
            wide_w, wide_x, ((1,), (1,))
        )
        for m in range(4):
            local = sort_leaf(4 * number + m, local)
        return local

    lax.fori_loop(0, 16, cluster, jnp.int32(0), unroll=UP_UNROLL)
    save = pltpu.make_async_copy(weights, weights_out, semaphores.at[5])
    save.start()
    for copy in copies[3:]:
        copy.wait()
    coefs = coef[:, 0:32]
    for block in range(4):
        halo[0:128, 32 * block : 32 * block + 32] = coefs[128 * block : 128 * block + 128]
    partial = dot3(top[...].reshape(512, 32), coefs, ((0,), (0,)))
    for block in range(4):
        halo[128:136, 32 * block : 32 * block + 32] = partial[8 * block : 8 * block + 8]
    for block in range(4):
        for i in range(4):
            halo[136 + 2 * block : 138 + 2 * block, 32 * i : 32 * i + 32] = proxy[4 * block + i]
    save.wait()


def near_loop(tasks, begin, count, place, columns, table, acc, spread, blocks):
    def decode(trip, u):
        index = trip * UNROLL + u
        task = tasks[begin + jnp.clip(index, 0, count - 1)]
        leaf = jnp.where((index >= 0) & (index < count), task >> 12, LPD)
        return leaf, task >> 12, place((task >> 6) & 63), task & (LPD - 1)

    def widen(trip):
        for u in range(UNROLL):
            _, _, slot, source = decode(trip, u)
            points = columns[pl.ds(pl.multiple_of(slot * 128, 128), 128), :]
            spread[u, 0:128, :] = lanes(points, 2 * source)
            spread[u, 128:256, :] = lanes(points, 2 * source + 1)

    def make(trip, target):
        for u in range(UNROLL):
            _, leaf, _, _ = decode(trip, u)
            row_x = target[pl.ds(2048 + 2 * leaf, 1), :]
            row_y = target[pl.ds(2049 + 2 * leaf, 1), :]
            kernel = decay(spread[u, 0:128, :] - row_x, spread[u, 128:256, :] - row_y)
            high, low = split(kernel)
            blocks[u, 0:128, :] = high
            blocks[u, 128:256, :] = low

    def multiply(trip):
        for u in range(UNROLL):
            leaf, _, slot, source = decode(trip, u)
            at = pl.multiple_of(slot * 2048 + 32 * source, 32)
            high, low = split(table[pl.ds(at, 32), :])
            left = jnp.concatenate(
                [
                    jnp.concatenate([high, high], axis=1),
                    jnp.concatenate([low, jnp.zeros_like(low)], axis=1),
                ],
                axis=0,
            )
            result = dot(left, blocks[u])
            rows = pl.ds(pl.multiple_of(32 * leaf, 32), 32)
            acc[rows, :] += result[0:32] + result[32:64]

    return widen, make, multiply


def near_run(count, widen, make, multiply, target):
    def step(trip, carry):
        multiply(trip - 2)
        make(trip - 1, target)
        widen(trip)
        return carry

    lax.fori_loop(0, count // UNROLL + 2, step, 0)


def local_kernel(begin, count, *refs):
    tasks, pack = refs[:2]
    before = refs[2] if begin else None
    out, acc, spread, blocks, columns = refs[-5:]
    acc[0:2048, :] = before[...] if begin else jnp.zeros((2048, 128), f32)
    columns[...] = pack[2048:2176, :].T
    parts = near_loop(
        tasks, begin, count, lambda code: 0, columns, pack, acc, spread, blocks
    )
    near_run(count, *parts, pack)
    out[...] = acc[0:2048, :]


def remote_kernel(begin, count, tasks, pack, north, west, east, south, before, *refs):
    out, acc, spread, blocks, columns, table, slots = refs
    for number, (fetched, code) in enumerate(((north, 0), (west, 15), (east, 17), (south, 32))):
        slots[code] = number
        columns[128 * number : 128 * number + 128, :] = fetched[2048:2176, :].T
        table[2048 * number : 2048 * number + 2048, :] = fetched[0:2048, :]
    acc[0:2048, :] = before[...]
    parts = near_loop(
        tasks, begin, count, lambda code: slots[code], columns, table, acc, spread, blocks
    )
    near_run(count, *parts, pack)
    out[...] = acc[0:2048, :]


def far_kernel(device, far, left, own, right, out):
    me = device[0]
    sources = [left[...], own[...], right[...]]
    stacked = jnp.concatenate(
        [h[0:128, 32 * g : 32 * g + 32] for h in sources for g in range(4)], axis=0
    )
    high, low = split(stacked)
    both = jnp.concatenate([high, low], axis=1)
    targets = own[136:144, :].T
    cluster_of = (
        lax.broadcasted_iota(jnp.int32, (16, 128), 0) * 4
        + lax.broadcasted_iota(jnp.int32, (16, 128), 1) // 32
    )
    for c in range(16):
        counts = jnp.zeros((16, 128), f32)
        for k in range(FAR):
            counts = counts + jnp.where(cluster_of == far[c, k] - (me - 1) * 16, 1.0, 0.0)
        rows = targets[32 * (c % 4) : 32 * (c % 4) + 32]
        lane = 2 * (c // 4)
        t_x = jnp.broadcast_to(rows[:, lane : lane + 1], (32, 128))
        t_y = jnp.broadcast_to(rows[:, lane + 1 : lane + 2], (32, 128))
        pieces = []
        for d in range(3):
            for g in range(4):
                s = sources[d][136 + 2 * g : 138 + 2 * g]
                pieces.append(
                    decay(t_x - s[0:1], t_y - s[1:2]) * counts[4 * d + g : 4 * d + g + 1]
                )
        kernel = jnp.concatenate(pieces, axis=1)
        k_high, k_low = split(kernel)
        first = dot(k_high, both)
        out[32 * c : 32 * c + 32, :] = first[:, 0:32] + first[:, 32:64] + dot(k_low, high)


def down_kernel(
    device, order, top_list, chip_map, piece_0, piece_1, piece_2, piece_3, proxy_top, top, low_part, weights, near, out, gathered, turned
):
    for number, piece in enumerate((piece_0, piece_1, piece_2, piece_3)):
        gathered[32 * number : 32 * number + 32] = piece[...]
    turned[...] = proxy_top[...].reshape(64, 128).T
    chip = device[0] // 2
    own_x, own_y, own_z = chip // 32, (chip // 8) % 4, chip % 8
    t_x = lanes(proxy_top[0], chip)
    t_y = lanes(proxy_top[1], chip)
    kernels = []
    rights = []
    for j in range(7):
        coordinates = []
        for i in range(4):
            k = min(4 * j + i, FAR - 1)
            source = chip_map[top_list[0, k]]
            coordinates.append(turned[pl.ds(source, 1), :])
            away_x = (own_x - source // 32 + 4) % 4
            away_y = (own_y - (source // 8) % 4 + 4) % 4
            away_z = (own_z - source % 8 + 8) % 8
            slot = (away_x * 4 + away_y) * 8 + away_z
            block = gathered[pl.ds(slot, 1)].reshape(8, 128)
            for g in range(4):
                rights.append(block[:, 32 * g : 32 * g + 32])
        s_x = jnp.concatenate([row[:, 0:32] for row in coordinates], axis=1)
        s_y = jnp.concatenate([row[:, 32:64] for row in coordinates], axis=1)
        kernel = decay(t_x - s_x, t_y - s_y)
        if 4 * j + 4 > FAR:
            used = lax.broadcasted_iota(jnp.int32, (32, 128), 1) < 32 * (FAR - 4 * j)
            kernel = jnp.where(used, kernel, 0.0)
        kernels.append(kernel)
    down_top = dot3(jnp.concatenate(kernels, axis=1), jnp.concatenate(rights, axis=0))
    down_low = low_part[...] + dot3(top[...].reshape(512, 32), down_top)
    for c in range(16):
        left = down_low[32 * c : 32 * c + 32].T
        right = jnp.concatenate(
            [weights[128 * c + 32 * m : 128 * c + 32 * m + 32, :] for m in range(4)], axis=1
        )
        result = dot3(left, right)
        for m in range(4):
            b = 4 * c + m
            columns = pl.ds(pl.multiple_of(order[b] * LEAF, LEAF), LEAF)
            out[:, columns] = result[:, 128 * m : 128 * m + 128] + near[32 * b : 32 * b + 32, :]


def call(body, out_shape, in_specs, out_specs, flops, mib, scratch=(), aliases=None):
    return pl.pallas_call(
        body,
        out_shape=out_shape,
        in_specs=in_specs,
        out_specs=out_specs,
        scratch_shapes=list(scratch),
        input_output_aliases=aliases or {},
        compiler_params=pltpu.CompilerParams(vmem_limit_bytes=mib * MIB),
        cost_estimate=pl.CostEstimate(flops=flops, bytes_accessed=0, transcendentals=0),
    )


def shape(*dims, dtype=f32):
    return jax.ShapeDtypeStruct(dims, dtype)


def device_shift(x, by, same_row):
    count = 256
    pairs = [
        (i, i + by)
        for i in range(count)
        if 0 <= i + by < count and (not same_row or i // 16 == (i + by) // 16)
    ]
    return lax.ppermute(x, AXES, pairs)


def chip_shift(x, by, size, stride):
    pairs = []
    for i in range(128):
        at = (i // stride) % size
        pairs.append((i, i + ((at + by) % size - at) * stride))
    return lax.ppermute(x, "leaf", pairs)


LOCAL_PARTS = (112, 104, 104)
REMOTE_PARTS = (128, 128)
MICRO = 2000000


def product(
    points,
    right_sides,
    leaf_order,
    leaf_basis,
    transfer_low,
    transfer_top,
    proxy_low,
    proxy_top,
    near_lists,
    far_lists,
    top_lists,
    subtree_map,
):
    device = lax.axis_index("leaf") * 2 + lax.axis_index("sub")
    device = device.astype(jnp.int32).reshape(1)
    pack = call(
        pack_kernel,
        shape(WINDOW, 128),
        [HBM, HBM, HBM],
        VMEM,
        2 * MICRO,
        62,
        [
            pltpu.SMEM((LPD,), jnp.int32),
            pltpu.VMEM((2, LPD * LEAF), f32),
            pltpu.VMEM((RHS, LPD * LEAF), f32),
            pltpu.SemaphoreType.DMA((3,)),
        ],
    )(leaf_order, points, right_sides)
    up = device_shift(pack, 16, False)
    down = device_shift(pack, -16, False)
    right = device_shift(pack, 1, True)
    left = device_shift(pack, -1, True)

    halo, weights, tasks = call(
        up_kernel,
        (shape(144, 128), shape(2048, 128), shape(LIST, dtype=jnp.int32)),
        [SMEM, HBM, VMEM, HBM, HBM, HBM, HBM],
        (VMEM, HBM, SMEM),
        4 * MICRO,
        62,
        [
            pltpu.SMEM((NEAR, LPD), jnp.int32),
            pltpu.VMEM((LPD, RANK, LEAF), f32),
            pltpu.VMEM((16, RANK, 128), f32),
            pltpu.VMEM((16, RANK, RANK), f32),
            pltpu.VMEM((16, 2, RANK), f32),
            pltpu.VMEM((2048, 128), f32),
            pltpu.VMEM((512, 128), f32),
            pltpu.SemaphoreType.DMA((6,)),
        ],
    )(device, near_lists.T, pack, leaf_basis, transfer_low, transfer_top, proxy_low)
    halo_left = device_shift(halo, 1, False)
    halo_right = device_shift(halo, -1, False)

    scratch = [
        pltpu.VMEM((2080, 128), f32),
        pltpu.VMEM((UNROLL, 256, 128), f32),
        pltpu.VMEM((UNROLL, 256, 128), bf16),
    ]
    near = None
    begin = 0
    for count in LOCAL_PARTS:

        def body(*refs, begin=begin, count=count):
            local_kernel(begin, count, *refs)

        operands = (tasks, pack) + ((near,) if begin else ())
        begin += count
        near = call(
            body,
            shape(2048, 128),
            [SMEM] + [VMEM] * (len(operands) - 1),
            VMEM,
            3 * MICRO,
            12,
            scratch + [pltpu.VMEM((128, 128), f32)],
        )(*operands)

    low_part = call(
        far_kernel, shape(512, 32), [SMEM, SMEM, VMEM, VMEM, VMEM], VMEM, 4 * MICRO, 12
    )(device, far_lists, halo_left, halo, halo_right)

    sibling = jnp.where(lax.axis_index("sub") == 0, halo_right[128:136], halo_left[128:136])
    gathered = (halo[128:136] + sibling).reshape(1, 8, 128)
    for number in range(3):
        other = chip_shift(gathered, 1 << number, 8, 1)
        gathered = jnp.concatenate([gathered, other], axis=0)
    pieces = [gathered]
    for by in range(1, 4):
        pieces.append(chip_shift(gathered, by, 4, 8))
    gathered = jnp.concatenate(pieces, axis=0)
    pieces = [gathered]
    for by in range(1, 4):
        pieces.append(chip_shift(gathered, by, 4, 32))

    for count in REMOTE_PARTS:

        def body(*refs, begin=begin, count=count):
            remote_kernel(begin, count, *refs)

        begin += count
        near = call(
            body,
            shape(2048, 128),
            [SMEM] + [VMEM] * 6,
            VMEM,
            4 * MICRO,
            24,
            scratch
            + [
                pltpu.VMEM((512, 128), f32),
                pltpu.VMEM((8192, 128), f32),
                pltpu.SMEM((64,), jnp.int32),
            ],
        )(tasks, pack, up, right, left, down, near)

    return call(
        down_kernel,
        shape(RHS, LPD * LEAF),
        [SMEM] * 4 + [VMEM] * 9,
        VMEM,
        4 * MICRO,
        20,
        [pltpu.VMEM((128, 8, 128), f32), pltpu.VMEM((128, 64), f32)],
    )(
        device,
        leaf_order,
        top_lists,
        subtree_map,
        *pieces,
        proxy_top.transpose(1, 2, 0),
        transfer_top,
        low_part,
        weights,
        near,
    )


def solution(mesh):
    return jax.shard_map(
        product,
        mesh=mesh,
        in_specs=(
            P(None, ("leaf", "sub")),
            P(None, ("leaf", "sub")),
            P(("leaf", "sub")),
            P(("leaf", "sub"), None, None),
            P(("leaf", "sub"), None, None),
            P(("leaf", "sub"), None, None),
            P(("leaf", "sub"), None, None),
            P(),
            P(("leaf", "sub"), None),
            P(("leaf", "sub"), None),
            P("leaf", None),
            P(),
        ),
        out_specs=P(None, ("leaf", "sub")),
        check_vma=False,
    )
```

profile of v0, /device:TPU:1, one launch (start us, length us, event | category | flops | bytes accessed | tf_op | source)
XLA Modules:
  0.0 119.5 jit_solution(13278126365874043046)
XLA Ops:
  0.0 2.5 %shard_map.118.pack.refs_1_ = f32[2176,128]{1,0:T(8,128)} custom-call(s32[64]{0:T(128)} %order.1, f32[2,8192]{1,0:T(2,128)} %points_in.1, f32[32,8192]{1,0:T(8,128)} %values_in.1), custom_call_target="tpu_custom_call" | custom-call | flops 4000000 | tf_op jit(solution)/shard_map/pallas_call | solution.py:375
  2.5 8.7 %shard_map.119 = (f32[144,128]{1,0:T(8,128)}, f32[2048,128]{1,0:T(8,128)}, s32[640]{0:T(1024)}) custom-call(s32[1]{0:T(128)} %bitcast.device, s32[9,64]{1,0:T(8,128)} %bitcast.7, f32[2176,128]{1,0:T(8,128)} %shard_map.118.pack.refs_1_, f32[64,32,128]{2,1,0:T(8,128)} %basis_in.1, f32[16,32,128]{2,1,0:T(8,128)} %low_in.1, f32[16,32,32]{2,1,0:T(8,128)} %top.1, ...), custom_call_target="tpu_custom_call" | custom-call | flops 8000000 | tf_op jit(solution)/shard_map/pallas_call | solution.py:394
  11.2 5.1 %collective-permute-start = (f32[144,128]{1,0:T(8,128)}, f32[144,128]{1,0:T(8,128)S(1)}, u32[]{:S(2)}, u32[]{:S(2)}) collective-permute-start(f32[144,128]{1,0:T(8,128)} %get-tuple-element.8.own), channel_id=1, source_target_pairs={{1,0},{2,1},{3,2},{4,3},{5,4},{6,5},{7,6},{8,7},{9,8},{10,9},{11,1... | collective-permute-start | bytes 221192 | tf_op jit(solution)/shard_map/ppermute | solution.py:343
  16.3 1.9 %collective-permute-start.1 = (f32[144,128]{1,0:T(8,128)}, f32[144,128]{1,0:T(8,128)S(1)}, u32[]{:S(2)}, u32[]{:S(2)}) collective-permute-start(f32[144,128]{1,0:T(8,128)} %get-tuple-element.8.own), channel_id=1, source_target_pairs={{0,1},{1,2},{2,3},{3,4},{4,5},{5,6},{6,7},{7,8},{8,9},{9,10},{10,1... | collective-permute-start | bytes 221192 | tf_op jit(solution)/shard_map/ppermute | solution.py:343
  18.2 3.1 %collective-permute-start.11 = (f32[2176,128]{1,0:T(8,128)S(1)}, f32[2176,128]{1,0:T(8,128)S(1)}, u32[]{:S(2)}, u32[]{:S(2)}) collective-permute-start(f32[2176,128]{1,0:T(8,128)S(1)} %copy-done), channel_id=1, source_target_pairs={{0,16},{1,17},{2,18},{3,19},{4,20},{5,21},{6,22},{7,23},{8,24},{9,... | collective-permute-start | bytes 3342344 | tf_op jit(solution)/shard_map/ppermute | solution.py:343
  21.3 2.7 %collective-permute-start.12 = (f32[2176,128]{1,0:T(8,128)S(1)}, f32[2176,128]{1,0:T(8,128)}, u32[]{:S(2)}, u32[]{:S(2)}) collective-permute-start(f32[2176,128]{1,0:T(8,128)S(1)} %copy-done), channel_id=1, source_target_pairs={{0,1},{1,2},{2,3},{3,4},{4,5},{5,6},{6,7},{7,8},{8,9},{9,10},{10,1... | collective-permute-start | bytes 3342344 | tf_op jit(solution)/shard_map/ppermute | solution.py:343
  24.7 1.6 %collective-permute-start.2 = (f32[1,8,128]{2,1,0:T(8,128)S(1)}, f32[1,8,128]{2,1,0:T(8,128)S(1)}, u32[]{:S(2)}, u32[]{:S(2)}) collective-permute-start(f32[1,8,128]{2,1,0:T(8,128)S(1)} %get-tuple-element.12), channel_id=1, source_target_pairs={{0,2},{2,4},{4,6},{6,8},{8,10},{10,12},{12,14},{14,0},{16,18},{18,... | collective-permute-start | bytes 12296 | tf_op jit(solution)/shard_map/ppermute | solution.py:351
  26.4 3.8 %collective-permute-start.13 = (f32[2176,128]{1,0:T(8,128)S(1)}, f32[2176,128]{1,0:T(8,128)S(1)}, u32[]{:S(2)}, u32[]{:S(2)}) collective-permute-start(f32[2176,128]{1,0:T(8,128)S(1)} %copy-done), channel_id=1, source_target_pairs={{1,0},{2,1},{3,2},{4,3},{5,4},{6,5},{7,6},{8,7},{9,8},{10,9},{11,1... | collective-permute-start | bytes 3342344 | tf_op jit(solution)/shard_map/ppermute | solution.py:343
  31.5 5.3 %collective-permute-done.2 = f32[1,8,128]{2,1,0:T(8,128)S(1)} collective-permute-done((f32[1,8,128]{2,1,0:T(8,128)S(1)}, f32[1,8,128]{2,1,0:T(8,128)S(1)}, u32[]{:S(2)}, u32[]{:S(2)}) %collective-permute-start.2) | collective-permute-done | bytes 4128 | tf_op jit(solution)/shard_map/ppermute | solution.py:351
  36.7 3.6 %collective-permute-start.3 = (f32[2,8,128]{2,1,0:T(8,128)S(1)}, f32[2,8,128]{2,1,0:T(8,128)S(1)}, u32[]{:S(2)}, u32[]{:S(2)}) collective-permute-start(f32[2,8,128]{2,1,0:T(8,128)S(1)} %pad_maximum_fusion.2), channel_id=1, source_target_pairs={{0,4},{2,6},{4,8},{6,10},{8,12},{10,14},{12,0},{14,2},{16,20},{18,... | collective-permute-start | bytes 24584 | tf_op jit(solution)/shard_map/ppermute | solution.py:351
  40.3 4.1 %collective-permute-done.3 = f32[2,8,128]{2,1,0:T(8,128)S(1)} collective-permute-done((f32[2,8,128]{2,1,0:T(8,128)S(1)}, f32[2,8,128]{2,1,0:T(8,128)S(1)}, u32[]{:S(2)}, u32[]{:S(2)}) %collective-permute-start.3) | collective-permute-done | bytes 8224 | tf_op jit(solution)/shard_map/ppermute | solution.py:351
  44.4 5.8 %collective-permute-start.4 = (f32[4,8,128]{2,1,0:T(8,128)S(1)}, f32[4,8,128]{2,1,0:T(8,128)S(1)}, u32[]{:S(2)}, u32[]{:S(2)}) collective-permute-start(f32[4,8,128]{2,1,0:T(8,128)S(1)} %pad_maximum_fusion.1), channel_id=1, source_target_pairs={{0,8},{2,10},{4,12},{6,14},{8,0},{10,2},{12,4},{14,6},{16,24},{18,... | collective-permute-start | bytes 49160 | tf_op jit(solution)/shard_map/ppermute | solution.py:351
  52.4 2.9 %collective-permute-done.5 = f32[8,8,128]{2,1,0:T(8,128)S(1)} collective-permute-done((f32[8,8,128]{2,1,0:T(8,128)S(1)}, f32[8,8,128]{2,1,0:T(8,128)S(1)}, u32[]{:S(2)}, u32[]{:S(2)}) %collective-permute-start.5) | collective-permute-done | bytes 32800 | tf_op jit(solution)/shard_map/ppermute | solution.py:351
  56.8 2.8 %collective-permute-done.6 = f32[8,8,128]{2,1,0:T(8,128)S(1)} collective-permute-done((f32[8,8,128]{2,1,0:T(8,128)S(1)}, f32[8,8,128]{2,1,0:T(8,128)S(1)}, u32[]{:S(2)}, u32[]{:S(2)}) %collective-permute-start.6) | collective-permute-done | bytes 32800 | tf_op jit(solution)/shard_map/ppermute | solution.py:351
  59.6 2.4 %collective-permute-start.7 = (f32[8,8,128]{2,1,0:T(8,128)S(1)}, f32[8,8,128]{2,1,0:T(8,128)S(1)}, u32[]{:S(2)}, u32[]{:S(2)}) collective-permute-start(f32[8,8,128]{2,1,0:T(8,128)S(1)} %pad_maximum_fusion), channel_id=1, source_target_pairs={{0,48},{2,50},{4,52},{6,54},{8,56},{10,58},{12,60},{14,62},{16,0},... | collective-permute-start | bytes 98312 | tf_op jit(solution)/shard_map/ppermute | solution.py:351
  62.0 1.8 %collective-permute-done.7 = f32[8,8,128]{2,1,0:T(8,128)S(1)} collective-permute-done((f32[8,8,128]{2,1,0:T(8,128)S(1)}, f32[8,8,128]{2,1,0:T(8,128)S(1)}, u32[]{:S(2)}, u32[]{:S(2)}) %collective-permute-start.7) | collective-permute-done | bytes 32800 | tf_op jit(solution)/shard_map/ppermute | solution.py:351
  63.8 6.3 %collective-permute-start.10 = (f32[32,8,128]{2,1,0:T(8,128)S(1)}, f32[32,8,128]{2,1,0:T(8,128)S(1)}, u32[]{:S(2)}, u32[]{:S(2)}) collective-permute-start(f32[32,8,128]{2,1,0:T(8,128)S(1)} %constant_dynamic-update-slice_fusion.piece_0), channel_id=1, source_target_pairs={{0,192},{2,194},{4,196},{6,198},{8,200},{10,202},{12,204},{14,206}... | collective-permute-start | bytes 393224 | tf_op jit(solution)/shard_map/ppermute | solution.py:351
  72.3 7.4 %shard_map.121.refs_2_ = f32[2048,128]{1,0:T(8,128)S(1)} custom-call(s32[640]{0:T(1024)S(1)} %copy-done.3, f32[2176,128]{1,0:T(8,128)S(1)} %copy-done), custom_call_target="tpu_custom_call" | custom-call | flops 6000000 | tf_op jit(solution)/shard_map/pallas_call | solution.py:429
  79.6 7.0 %shard_map.122.refs_2_ = f32[2048,128]{1,0:T(8,128)S(1)} custom-call(s32[640]{0:T(1024)S(1)} %copy-done.3, f32[2176,128]{1,0:T(8,128)S(1)} %copy-done, f32[2048,128]{1,0:T(8,128)S(1)} %shard_map.121.refs_2_), custom_call_target="tpu_custom_call" | custom-call | flops 6000000 | tf_op jit(solution)/shard_map/pallas_call | solution.py:429
  86.7 7.0 %shard_map.123.refs_6_ = f32[2048,128]{1,0:T(8,128)S(1)} custom-call(s32[640]{0:T(1024)S(1)} %copy-done.3, f32[2176,128]{1,0:T(8,128)S(1)} %copy-done, f32[2048,128]{1,0:T(8,128)S(1)} %shard_map.122.refs_2_), custom_call_target="tpu_custom_call" | custom-call | flops 6000000 | tf_op jit(solution)/shard_map/pallas_call | solution.py:429
  93.7 3.4 %shard_map.120.low_part = f32[512,32]{1,0:T(8,128)S(1)} custom-call(s32[1]{0:T(128)} %bitcast.device, s32[16,27]{1,0:T(8,128)S(1)} %copy-done.6, f32[144,128]{1,0:T(8,128)S(1)} %collective-permute-done.1.left, f32[144,128]{1,0:T(8,128)S(1)} %copy-done.4, f32[144,128]{1,0:T(8,128)S(1)} %collective-permute-done.right), custom_call_target="tpu_custom_call" | custom-call | flops 8000000 | tf_op jit(solution)/shard_map/pallas_call | solution.py:439
  97.2 9.3 %shard_map.124.refs_6_ = f32[2048,128]{1,0:T(8,128)S(1)} custom-call(s32[640]{0:T(1024)S(1)} %copy-done.3, f32[2176,128]{1,0:T(8,128)S(1)} %copy-done, f32[2176,128]{1,0:T(8,128)S(1)} %collective-permute-done.11.refs_2_, f32[2176,128]{1,0:T(8,128)} %collective-permute-done.12.refs_3_, f32[2176,128]{1,0:T(8,128)S(1)} %collective-permute-done.13.refs_4_, ...), custom_call_target="tpu_custom_call" | custom-call | flops 8000000 | tf_op jit(solution)/shard_map/pallas_call | solution.py:462
  106.6 9.4 %shard_map.125.near = f32[2048,128]{1,0:T(8,128)S(1)} custom-call(s32[640]{0:T(1024)S(1)} %copy-done.3, f32[2176,128]{1,0:T(8,128)S(1)} %copy-done, f32[2176,128]{1,0:T(8,128)S(1)} %collective-permute-done.11.refs_2_, f32[2176,128]{1,0:T(8,128)} %collective-permute-done.12.refs_3_, f32[2176,128]{1,0:T(8,128)S(1)} %collective-permute-done.13.refs_4_, ...), custom_call_target="tpu_custom_call" | custom-call | flops 8000000 | tf_op jit(solution)/shard_map/pallas_call | solution.py:462
  116.1 3.4 %shard_map.126 = f32[32,8192]{1,0:T(8,128)} custom-call(s32[1]{0:T(128)} %bitcast.device, s32[64]{0:T(128)S(1)} %copy-done.7, s32[1,27]{1,0:T(1,128)S(1)} %copy-done.8, s32[128]{0:T(128)S(1)} %copy-done.9, f32[32,8,128]{2,1,0:T(8,128)S(1)} %constant_dynamic-update-slice_fusion.piece_0, f32[32,8,128]{2,1,0:T(8,128)S(1)} %collective-permute-done.8.piece_1, ...), custom_call_target="tpu_custom_call" | custom-call | flops 8000000 | tf_op jit(solution)/shard_map/pallas_call | solution.py:477
  (45 shorter events, 7.9 us)
Async XLA Ops:
  2.5 15.7 %copy-start = (f32[2176,128]{1,0:T(8,128)S(1)}, f32[2176,128]{1,0:T(8,128)}, u32[]{:S(2)}) copy-start(f32[2176,128]{1,0:T(8,128)} %shard_map.118.pack.refs_1_) | copy-start | bytes 3342340
  11.2 12.8 %collective-permute-start = (f32[144,128]{1,0:T(8,128)}, f32[144,128]{1,0:T(8,128)S(1)}, u32[]{:S(2)}, u32[]{:S(2)}) collective-permute-start(f32[144,128]{1,0:T(8,128)} %get-tuple-element.8.own), channel_id=1, source_target_pairs={{1,0},{2,1},{3,2},{4,3},{5,4},{6,5},{7,6},{8,7},{9,8},{10,9},{11,1... | collective-permute-start | bytes 221192 | tf_op jit(solution)/shard_map/ppermute | solution.py:343
  16.3 7.7 %collective-permute-start.1 = (f32[144,128]{1,0:T(8,128)}, f32[144,128]{1,0:T(8,128)S(1)}, u32[]{:S(2)}, u32[]{:S(2)}) collective-permute-start(f32[144,128]{1,0:T(8,128)} %get-tuple-element.8.own), channel_id=1, source_target_pairs={{0,1},{1,2},{2,3},{3,4},{4,5},{5,6},{6,7},{7,8},{8,9},{9,10},{10,1... | collective-permute-start | bytes 221192 | tf_op jit(solution)/shard_map/ppermute | solution.py:343
  18.2 51.9 %collective-permute-start.11 = (f32[2176,128]{1,0:T(8,128)S(1)}, f32[2176,128]{1,0:T(8,128)S(1)}, u32[]{:S(2)}, u32[]{:S(2)}) collective-permute-start(f32[2176,128]{1,0:T(8,128)S(1)} %copy-done), channel_id=1, source_target_pairs={{0,16},{1,17},{2,18},{3,19},{4,20},{5,21},{6,22},{7,23},{8,24},{9,... | collective-permute-start | bytes 3342344 | tf_op jit(solution)/shard_map/ppermute | solution.py:343
  21.3 48.8 %collective-permute-start.12 = (f32[2176,128]{1,0:T(8,128)S(1)}, f32[2176,128]{1,0:T(8,128)}, u32[]{:S(2)}, u32[]{:S(2)}) collective-permute-start(f32[2176,128]{1,0:T(8,128)S(1)} %copy-done), channel_id=1, source_target_pairs={{0,1},{1,2},{2,3},{3,4},{4,5},{5,6},{6,7},{7,8},{8,9},{9,10},{10,1... | collective-permute-start | bytes 3342344 | tf_op jit(solution)/shard_map/ppermute | solution.py:343
  24.7 12.0 %collective-permute-start.2 = (f32[1,8,128]{2,1,0:T(8,128)S(1)}, f32[1,8,128]{2,1,0:T(8,128)S(1)}, u32[]{:S(2)}, u32[]{:S(2)}) collective-permute-start(f32[1,8,128]{2,1,0:T(8,128)S(1)} %get-tuple-element.12), channel_id=1, source_target_pairs={{0,2},{2,4},{4,6},{6,8},{8,10},{10,12},{12,14},{14,0},{16,18},{18,... | collective-permute-start | bytes 12296 | tf_op jit(solution)/shard_map/ppermute | solution.py:351
  26.4 70.8 %collective-permute-start.13 = (f32[2176,128]{1,0:T(8,128)S(1)}, f32[2176,128]{1,0:T(8,128)S(1)}, u32[]{:S(2)}, u32[]{:S(2)}) collective-permute-start(f32[2176,128]{1,0:T(8,128)S(1)} %copy-done), channel_id=1, source_target_pairs={{1,0},{2,1},{3,2},{4,3},{5,4},{6,5},{7,6},{8,7},{9,8},{10,9},{11,1... | collective-permute-start | bytes 3342344 | tf_op jit(solution)/shard_map/ppermute | solution.py:343
  30.2 67.0 %collective-permute-start.14 = (f32[2176,128]{1,0:T(8,128)S(1)}, f32[2176,128]{1,0:T(8,128)S(1)}, u32[]{:S(2)}, u32[]{:S(2)}) collective-permute-start(f32[2176,128]{1,0:T(8,128)S(1)} %copy-done), channel_id=1, source_target_pairs={{16,0},{17,1},{18,2},{19,3},{20,4},{21,5},{22,6},{23,7},{24,8},{25... | collective-permute-start | bytes 3342344 | tf_op jit(solution)/shard_map/ppermute | solution.py:343
  36.7 7.6 %collective-permute-start.3 = (f32[2,8,128]{2,1,0:T(8,128)S(1)}, f32[2,8,128]{2,1,0:T(8,128)S(1)}, u32[]{:S(2)}, u32[]{:S(2)}) collective-permute-start(f32[2,8,128]{2,1,0:T(8,128)S(1)} %pad_maximum_fusion.2), channel_id=1, source_target_pairs={{0,4},{2,6},{4,8},{6,10},{8,12},{10,14},{12,0},{14,2},{16,20},{18,... | collective-permute-start | bytes 24584 | tf_op jit(solution)/shard_map/ppermute | solution.py:351
  44.4 7.0 %collective-permute-start.4 = (f32[4,8,128]{2,1,0:T(8,128)S(1)}, f32[4,8,128]{2,1,0:T(8,128)S(1)}, u32[]{:S(2)}, u32[]{:S(2)}) collective-permute-start(f32[4,8,128]{2,1,0:T(8,128)S(1)} %pad_maximum_fusion.1), channel_id=1, source_target_pairs={{0,8},{2,10},{4,12},{6,14},{8,0},{10,2},{12,4},{14,6},{16,24},{18,... | collective-permute-start | bytes 49160 | tf_op jit(solution)/shard_map/ppermute | solution.py:351
  51.3 4.0 %collective-permute-start.5 = (f32[8,8,128]{2,1,0:T(8,128)S(1)}, f32[8,8,128]{2,1,0:T(8,128)S(1)}, u32[]{:S(2)}, u32[]{:S(2)}) collective-permute-start(f32[8,8,128]{2,1,0:T(8,128)S(1)} %pad_maximum_fusion), channel_id=1, source_target_pairs={{0,16},{2,18},{4,20},{6,22},{8,24},{10,26},{12,28},{14,30},{16,32}... | collective-permute-start | bytes 98312 | tf_op jit(solution)/shard_map/ppermute | solution.py:351
  55.3 4.3 %collective-permute-start.6 = (f32[8,8,128]{2,1,0:T(8,128)S(1)}, f32[8,8,128]{2,1,0:T(8,128)S(1)}, u32[]{:S(2)}, u32[]{:S(2)}) collective-permute-start(f32[8,8,128]{2,1,0:T(8,128)S(1)} %pad_maximum_fusion), channel_id=1, source_target_pairs={{0,32},{2,34},{4,36},{6,38},{8,40},{10,42},{12,44},{14,46},{16,48}... | collective-permute-start | bytes 98312 | tf_op jit(solution)/shard_map/ppermute | solution.py:351
  59.6 4.2 %collective-permute-start.7 = (f32[8,8,128]{2,1,0:T(8,128)S(1)}, f32[8,8,128]{2,1,0:T(8,128)S(1)}, u32[]{:S(2)}, u32[]{:S(2)}) collective-permute-start(f32[8,8,128]{2,1,0:T(8,128)S(1)} %pad_maximum_fusion), channel_id=1, source_target_pairs={{0,48},{2,50},{4,52},{6,54},{8,56},{10,58},{12,60},{14,62},{16,0},... | collective-permute-start | bytes 98312 | tf_op jit(solution)/shard_map/ppermute | solution.py:351
  63.8 52.2 %collective-permute-start.10 = (f32[32,8,128]{2,1,0:T(8,128)S(1)}, f32[32,8,128]{2,1,0:T(8,128)S(1)}, u32[]{:S(2)}, u32[]{:S(2)}) collective-permute-start(f32[32,8,128]{2,1,0:T(8,128)S(1)} %constant_dynamic-update-slice_fusion.piece_0), channel_id=1, source_target_pairs={{0,192},{2,194},{4,196},{6,198},{8,200},{10,202},{12,204},{14,206}... | collective-permute-start | bytes 393224 | tf_op jit(solution)/shard_map/ppermute | solution.py:351
  70.2 45.9 %collective-permute-start.8 = (f32[32,8,128]{2,1,0:T(8,128)S(1)}, f32[32,8,128]{2,1,0:T(8,128)S(1)}, u32[]{:S(2)}, u32[]{:S(2)}) collective-permute-start(f32[32,8,128]{2,1,0:T(8,128)S(1)} %constant_dynamic-update-slice_fusion.piece_0), channel_id=1, source_target_pairs={{0,64},{2,66},{4,68},{6,70},{8,72},{10,74},{12,76},{14,78},{16,80}... | collective-permute-start | bytes 393224 | tf_op jit(solution)/shard_map/ppermute | solution.py:351
  70.2 45.9 %collective-permute-start.9 = (f32[32,8,128]{2,1,0:T(8,128)S(1)}, f32[32,8,128]{2,1,0:T(8,128)S(1)}, u32[]{:S(2)}, u32[]{:S(2)}) collective-permute-start(f32[32,8,128]{2,1,0:T(8,128)S(1)} %constant_dynamic-update-slice_fusion.piece_0), channel_id=1, source_target_pairs={{0,128},{2,130},{4,132},{6,134},{8,136},{10,138},{12,140},{14,142}... | collective-permute-start | bytes 393224 | tf_op jit(solution)/shard_map/ppermute | solution.py:351
  86.7 7.1 %copy-start.4 = (f32[144,128]{1,0:T(8,128)S(1)}, f32[144,128]{1,0:T(8,128)}, u32[]{:S(2)}) copy-start(f32[144,128]{1,0:T(8,128)} %get-tuple-element.8.own) | copy-start | bytes 221188
  86.7 7.1 %copy-start.6 = (s32[16,27]{1,0:T(8,128)S(1)}, s32[16,27]{1,0:T(8,128)}, u32[]{:S(2)}) copy-start(s32[16,27]{1,0:T(8,128)} %far.1) | copy-start | bytes 5188
  106.5 9.5 %copy-start.1 = (f32[2048,128]{1,0:T(8,128)S(1)}, f32[2048,128]{1,0:T(8,128)}, u32[]{:S(2)}) copy-start(f32[2048,128]{1,0:T(8,128)} %get-tuple-element.9.weights) | copy-start | bytes 3145732
  106.5 9.5 %copy-start.2 = (f32[16,32,32]{2,1,0:T(8,128)S(1)}, f32[16,32,32]{2,1,0:T(8,128)}, u32[]{:S(2)}) copy-start(f32[16,32,32]{2,1,0:T(8,128)} %top.1) | copy-start | bytes 196612
  106.5 9.5 %copy-start.5 = (f32[128,2,32]{0,2,1:T(8,128)S(1)}, f32[128,2,32]{0,2,1:T(8,128)}, u32[]{:S(2)}) copy-start(f32[128,2,32]{0,2,1:T(8,128)} %param.19) | copy-start | bytes 98308
  106.5 9.5 %copy-start.7 = (s32[64]{0:T(128)S(1)}, s32[64]{0:T(128)}, u32[]{:S(2)}) copy-start(s32[64]{0:T(128)} %order.1) | copy-start | bytes 772
  106.6 9.5 %copy-start.8 = (s32[1,27]{1,0:T(1,128)S(1)}, s32[1,27]{1,0:T(1,128)}, u32[]{:S(2)}) copy-start(s32[1,27]{1,0:T(1,128)} %top_list.1) | copy-start | bytes 328
  106.6 9.5 %copy-start.9 = (s32[128]{0:T(128)S(1)}, s32[128]{0:T(128)}, u32[]{:S(2)}) copy-start(s32[128]{0:T(128)} %chip_map.1) | copy-start | bytes 1540
  (1 other events, 0.7 us)
where the time goes:
time: 122 us; the launch traced here: 120 us
  Pallas kernels  58.1 us (48%)
  starting transfers between devices  41.7 us (34%)
  waiting for transfers between devices  18 us (15%)
    ppermute x9, starting transfers between devices, chip_shift(): return lax.ppermute(x, 'leaf', pairs)  23.8 us
    pallas_call x3, Pallas kernels, product(): call(body, shape(2048, 128), [SMEM] + [VMEM] * (len(operands) - 1), VMEM,...  21.4 us
    pallas_call x2, Pallas kernels, product(): call(body, shape(2048, 128), [SMEM] + [VMEM] * 6, VMEM, 4 * MICRO, 24, sc...  18.8 us
    ppermute x9, waiting for transfers between devices, chip_shift(): return lax.ppermute(x, 'leaf', pairs)  18 us
    ppermute x6, starting transfers between devices, device_shift(): return lax.ppermute(x, AXES, pairs)  17.9 us
    pallas_call x1, Pallas kernels, product(): call(up_kernel, (shape(144, 128), shape(2048, 128), shape(LIST, dtype=jnp...  8.67 us
    pallas_call x1, Pallas kernels, product(): call(down_kernel, shape(RHS, LPD * LEAF), [SMEM] * 4 + [VMEM] * 9, VMEM,...  3.42 us
    pallas_call x1, Pallas kernels, product(): call(far_kernel, shape(512, 32), [SMEM, SMEM, VMEM, VMEM, VMEM], VMEM, 4...  3.4 us
  transfers between devices with their start and end apart: 15, of which 6 were waited for; matrix products, arithmetic and copies ran while one was open for 1% of the time, Pallas kernels for 36%

commit v1 on v0

v1 whole, which is shorter than its diff:
```python
import jax
import jax.numpy as jnp
import numpy as np
from jax import lax
from jax.experimental import pallas as pl
from jax.experimental.pallas import tpu as pltpu
from jax.sharding import PartitionSpec as P


LEAF = 128
RANK = 32
RHS = 32
LPD = 64
NEAR = 9
FAR = 27
LOCAL = LPD * NEAR - 256
UNROLL = 8
UP_UNROLL = 4
HALO_AT = 2176
BUNDLE = HALO_AT + 144
LIST = 640
AXES = ("leaf", "sub")
MIB = 1024 * 1024
RATE = float(-4.0 / np.log(2.0))
TINY = 1e-30
f32 = jnp.float32
bf16 = jnp.bfloat16
VMEM = pl.BlockSpec(memory_space=pltpu.VMEM)
SMEM = pl.BlockSpec(memory_space=pltpu.SMEM)
HBM = pl.BlockSpec(memory_space=pltpu.HBM)


def decay(delta_x, delta_y):
    square = jnp.maximum(delta_x * delta_x + delta_y * delta_y, TINY)
    return jnp.exp2((square * lax.rsqrt(square)) * RATE)


def split(x):
    high = x.astype(bf16)
    return high, (x - high.astype(f32)).astype(bf16)


def dot(a, b, contract=((1,), (0,))):
    return lax.dot_general(a, b, (contract, ((), ())), preferred_element_type=f32)


def dot3(a, b, contract=((1,), (0,))):
    a_high, a_low = split(a)
    b_high, b_low = split(b)
    return (
        dot(a_high, b_high, contract) + dot(a_high, b_low, contract) + dot(a_low, b_high, contract)
    )


def lanes(x, lane):
    index = jnp.full(x.shape, lane, jnp.int32)
    return jnp.take_along_axis(x, index, axis=1, mode="promise_in_bounds")


def fetch(pairs, semaphores):
    copies = [
        pltpu.make_async_copy(source, target, semaphores.at[number])
        for number, (source, target) in enumerate(pairs)
    ]
    for copy in copies:
        copy.start()
    return copies


def up_kernel(
    device,
    order_in,
    near_in,
    points_in,
    values_in,
    basis_in,
    low_in,
    top_in,
    proxy_in,
    bundle_out,
    weights_out,
    tasks,
    order,
    near,
    points,
    values,
    basis,
    low,
    top,
    proxy,
    weights,
    bundle,
    coef,
    semaphores,
):
    pairs = (
        (order_in, order),
        (near_in, near),
        (values_in, values),
        (points_in, points),
        (low_in, low),
        (basis_in, basis),
        (top_in, top),
        (proxy_in, proxy),
    )
    copies = fetch(pairs, semaphores)
    halo = bundle.at[pl.ds(HALO_AT, 144)]
    base = device[0] * LPD
    row_block = lax.broadcasted_iota(jnp.int32, (128, 128), 0) // 32
    lane_block = lax.broadcasted_iota(jnp.int32, (128, 128), 1) // 32
    diagonal = row_block == lane_block
    for copy in copies[:4]:
        copy.wait()
    for leaf in range(LPD):
        block = pl.ds(pl.multiple_of(order[leaf] * LEAF, LEAF), LEAF)
        bundle[32 * leaf : 32 * leaf + 32, :] = values[:, block]
        bundle[2048 + 2 * leaf : 2048 + 2 * leaf + 2, :] = points[:, block]

    def publish(at, rows, number):
        part = pl.ds(at, rows)
        return pltpu.make_async_copy(
            bundle.at[part], bundle_out.at[part], semaphores.at[12 + number]
        )

    publish(0, HALO_AT, 0).start()
    for copy in copies[4:6]:
        copy.wait()

    def save(part):
        rows = pl.ds(512 * part, 512)
        return pltpu.make_async_copy(
            weights.at[rows], weights_out.at[rows], semaphores.at[8 + part]
        )

    def sort_leaf(leaf, local):
        code = leaf * 4096 + 1024 - base
        for k in range(NEAR):
            entry = near[k, leaf]
            home = (entry >> 6) == device[0]
            where = jnp.where(home, local, (leaf * NEAR + (k + LOCAL)) - local)
            tasks[where] = entry + code
            local = local + home.astype(jnp.int32)
        return local

    def cluster(number, local):
        transfer = low[number]
        stacked = jnp.where(diagonal, jnp.concatenate([transfer] * 4, axis=0), 0.0)
        bases = basis[pl.ds(4 * number, 4)].reshape(128, LEAF)
        product = dot3(stacked, bases)
        rows = pl.ds(pl.multiple_of(128 * number, 128), 128)
        weights[rows, :] = product
        x = bundle[rows, :]
        wide_w = jnp.concatenate([product[32 * m : 32 * m + 32] for m in range(4)], axis=1)
        wide_x = jnp.concatenate([x[32 * m : 32 * m + 32] for m in range(4)], axis=1)
        coef[pl.ds(pl.multiple_of(32 * number, 32), 32), 0:32] = dot3(
            wide_w, wide_x, ((1,), (1,))
        )
        for m in range(4):
            local = sort_leaf(4 * number + m, local)
        return local

    local = jnp.int32(0)
    for part in range(4):
        local = lax.fori_loop(4 * part, 4 * part + 4, cluster, local, unroll=UP_UNROLL)
        save(part).start()
    for copy in copies[6:]:
        copy.wait()
    coefs = coef[:, 0:32]
    for block in range(4):
        halo[0:128, 32 * block : 32 * block + 32] = coefs[128 * block : 128 * block + 128]
    partial = dot3(top[...].reshape(512, 32), coefs, ((0,), (0,)))
    for block in range(4):
        halo[128:136, 32 * block : 32 * block + 32] = partial[8 * block : 8 * block + 8]
    for block in range(4):
        for i in range(4):
            halo[136 + 2 * block : 138 + 2 * block, 32 * i : 32 * i + 32] = proxy[4 * block + i]
    publish(HALO_AT, 144, 1).start()
    publish(0, HALO_AT, 0).wait()
    for part in range(4):
        save(part).wait()
    publish(HALO_AT, 144, 1).wait()


def near_run(tasks, begin, count, place, columns, table, target, acc, spread, blocks):
    def decode(trip, u):
        index = trip * UNROLL + u
        task = tasks[begin + jnp.clip(index, 0, count - 1)]
        leaf = jnp.where((index >= 0) & (index < count), task >> 12, LPD)
        return leaf, task >> 12, place((task >> 6) & 63), task & (LPD - 1)

    def widen(trip, u):
        _, _, slot, source = decode(trip, u)
        points = columns[pl.ds(pl.multiple_of(slot * 128, 128), 128), :]
        spread[u, 0:128, :] = lanes(points, 2 * source)
        spread[u, 128:256, :] = lanes(points, 2 * source + 1)

    def make(trip, u):
        _, leaf, _, _ = decode(trip, u)
        row_x = target[pl.ds(2048 + 2 * leaf, 1), :]
        row_y = target[pl.ds(2049 + 2 * leaf, 1), :]
        kernel = decay(spread[u, 0:128, :] - row_x, spread[u, 128:256, :] - row_y)
        high, low = split(kernel)
        blocks[u, 0:128, :] = high
        blocks[u, 128:256, :] = low

    def multiply(trip, u):
        leaf, _, slot, source = decode(trip, u)
        at = pl.multiple_of(slot * 2048 + 32 * source, 32)
        high, low = split(table[pl.ds(at, 32), :])
        left = jnp.concatenate(
            [
                jnp.concatenate([high, high], axis=1),
                jnp.concatenate([low, jnp.zeros_like(low)], axis=1),
            ],
            axis=0,
        )
        result = dot(left, blocks[u])
        rows = pl.ds(pl.multiple_of(32 * leaf, 32), 32)
        acc[rows, :] += result[0:32] + result[32:64]

    def step(trip, carry):
        for u in range(UNROLL):
            multiply(trip - 2, u)
            make(trip - 1, u)
            widen(trip, u)
        return carry

    lax.fori_loop(0, count // UNROLL + 2, step, 0)


def local_kernel(begin, count, *refs):
    tasks_in, pack = refs[:2]
    before = refs[2] if begin else None
    out, acc, spread, blocks, tasks, columns, semaphores = refs[-7:]
    (copy,) = fetch([(tasks_in, tasks)], semaphores)
    acc[0:2048, :] = before[...] if begin else jnp.zeros((2048, 128), f32)
    columns[...] = pack[2048:2176, :].T
    copy.wait()
    near_run(tasks, begin, count, lambda code: 0, columns, pack, pack, acc, spread, blocks)
    out[...] = acc[0:2048, :]


def remote_kernel(begin, count, device, tasks_in, pack, near_0, near_1, near_2, near_3, before, *refs):
    out, acc, spread, blocks, tasks, columns, table, points, slots, semaphores = refs
    fetched = (near_0, near_1, near_2, near_3)
    pairs = [(tasks_in, tasks)]
    for number in range(4):
        pairs.append((fetched[number].at[pl.ds(2048, 128)], points.at[pl.ds(128 * number, 128)]))
        pairs.append((fetched[number].at[pl.ds(0, 2048)], table.at[pl.ds(2048 * number, 2048)]))
    copies = fetch(pairs, semaphores)
    acc[0:2048, :] = before[...]
    row, column = (device[0] >> 4) & 1, device[0] & 1
    slots[0], slots[32] = 1 - row, row
    slots[15], slots[17] = 3 - column, 2 + column
    copies[0].wait()
    for number in range(4):
        copies[2 * number + 1].wait()
        columns[128 * number : 128 * number + 128, :] = points[
            128 * number : 128 * number + 128, :
        ].T
    for number in range(4):
        copies[2 * number + 2].wait()
    near_run(
        tasks, begin, count, lambda code: slots[code], columns, table, pack, acc, spread, blocks
    )
    out[...] = acc[0:2048, :]


def far_kernel(device, far_in, beside_in, own_in, across_in, out, far, halos, semaphores):
    me = device[0]
    pairs = [(far_in, far)]
    for number, bundle in enumerate((beside_in, own_in, across_in)):
        pairs.append((bundle.at[pl.ds(HALO_AT, 144)], halos.at[number]))
    for copy in fetch(pairs, semaphores):
        copy.wait()
    sources = [halos[0], halos[1], halos[2]]
    step = 16 - 32 * (me & 1)
    stacked = jnp.concatenate(
        [h[0:128, 32 * g : 32 * g + 32] for h in sources for g in range(4)], axis=0
    )
    high, low = split(stacked)
    both = jnp.concatenate([high, low], axis=1)
    targets = halos[1, 136:144, :].T
    row = lax.broadcasted_iota(jnp.int32, (16, 128), 0)
    side = 1 - jnp.minimum(row >> 2, 2)
    cluster_of = (
        me * 16 + side * step + (row & 3) * 4 + (lax.broadcasted_iota(jnp.int32, (16, 128), 1) >> 5)
    )
    for c in range(16):
        counts = jnp.zeros((16, 128), f32)
        for k in range(FAR):
            counts = counts + jnp.where(cluster_of == far[c, k], 1.0, 0.0)
        rows = targets[32 * (c % 4) : 32 * (c % 4) + 32]
        lane = 2 * (c // 4)
        t_x = jnp.broadcast_to(rows[:, lane : lane + 1], (32, 128))
        t_y = jnp.broadcast_to(rows[:, lane + 1 : lane + 2], (32, 128))
        pieces = []
        for d in range(3):
            for g in range(4):
                s = sources[d][136 + 2 * g : 138 + 2 * g]
                pieces.append(
                    decay(t_x - s[0:1], t_y - s[1:2]) * counts[4 * d + g : 4 * d + g + 1]
                )
        kernel = jnp.concatenate(pieces, axis=1)
        k_high, k_low = split(kernel)
        first = dot(k_high, both)
        out[32 * c : 32 * c + 32, :] = first[:, 0:32] + first[:, 32:64] + dot(k_low, high)


def down_kernel(
    device, order, top_list, chip_map, piece_0, piece_1, piece_2, piece_3, proxy_top, top, low_part, weights, near, out, gathered, turned
):
    for number, piece in enumerate((piece_0, piece_1, piece_2, piece_3)):
        gathered[32 * number : 32 * number + 32] = piece[...]
    turned[...] = proxy_top[...].reshape(64, 128).T
    chip = device[0] // 2
    t_x = lanes(proxy_top[0], chip)
    t_y = lanes(proxy_top[1], chip)
    kernels = []
    rights = []
    for j in range(7):
        coordinates = []
        for i in range(4):
            k = min(4 * j + i, FAR - 1)
            source = chip_map[top_list[0, k]]
            coordinates.append(turned[pl.ds(source, 1), :])
            slot = chip ^ source
            block = gathered[pl.ds(slot, 1)].reshape(8, 128)
            for g in range(4):
                rights.append(block[:, 32 * g : 32 * g + 32])
        s_x = jnp.concatenate([row[:, 0:32] for row in coordinates], axis=1)
        s_y = jnp.concatenate([row[:, 32:64] for row in coordinates], axis=1)
        kernel = decay(t_x - s_x, t_y - s_y)
        if 4 * j + 4 > FAR:
            used = lax.broadcasted_iota(jnp.int32, (32, 128), 1) < 32 * (FAR - 4 * j)
            kernel = jnp.where(used, kernel, 0.0)
        kernels.append(kernel)
    down_top = dot3(jnp.concatenate(kernels, axis=1), jnp.concatenate(rights, axis=0))
    down_low = low_part[...] + dot3(top[...].reshape(512, 32), down_top)
    for c in range(16):
        left = down_low[32 * c : 32 * c + 32].T
        right = jnp.concatenate(
            [weights[128 * c + 32 * m : 128 * c + 32 * m + 32, :] for m in range(4)], axis=1
        )
        result = dot3(left, right)
        for m in range(4):
            b = 4 * c + m
            columns = pl.ds(pl.multiple_of(order[b] * LEAF, LEAF), LEAF)
            out[:, columns] = result[:, 128 * m : 128 * m + 128] + near[32 * b : 32 * b + 32, :]


def call(body, out_shape, in_specs, out_specs, flops, mib, scratch=(), aliases=None):
    return pl.pallas_call(
        body,
        out_shape=out_shape,
        in_specs=in_specs,
        out_specs=out_specs,
        scratch_shapes=list(scratch),
        input_output_aliases=aliases or {},
        compiler_params=pltpu.CompilerParams(vmem_limit_bytes=mib * MIB),
        cost_estimate=pl.CostEstimate(flops=flops, bytes_accessed=0, transcendentals=0),
    )


def shape(*dims, dtype=f32):
    return jax.ShapeDtypeStruct(dims, dtype)


def swap(x, first, by, row):
    pairs = []
    for i in range(256):
        other = i + by
        if (i // by) % 2 == first and other < 256 and i // row == other // row:
            pairs += [(i, other), (other, i)]
    return lax.ppermute(x, AXES, pairs)


def chip_swap(x, bits):
    return lax.ppermute(x, "leaf", [(i, i ^ bits) for i in range(128)])


LOCAL_PARTS = (112, 104, 104)
REMOTE_PARTS = (256,)
MICRO = 2000000


def product(
    points,
    right_sides,
    leaf_order,
    leaf_basis,
    transfer_low,
    transfer_top,
    proxy_low,
    proxy_top,
    near_lists,
    far_lists,
    top_lists,
    subtree_map,
):
    device = lax.axis_index("leaf") * 2 + lax.axis_index("sub")
    device = device.astype(jnp.int32).reshape(1)
    pack, weights, tasks = call(
        up_kernel,
        (shape(BUNDLE, 128), shape(2048, 128), shape(LIST, dtype=jnp.int32)),
        [SMEM] + [HBM] * 8,
        (HBM, HBM, SMEM),
        4 * MICRO,
        62,
        [
            pltpu.SMEM((LPD,), jnp.int32),
            pltpu.SMEM((NEAR, LPD), jnp.int32),
            pltpu.VMEM((2, LPD * LEAF), f32),
            pltpu.VMEM((RHS, LPD * LEAF), f32),
            pltpu.VMEM((LPD, RANK, LEAF), f32),
            pltpu.VMEM((16, RANK, 128), f32),
            pltpu.VMEM((16, RANK, RANK), f32),
            pltpu.VMEM((16, 2, RANK), f32),
            pltpu.VMEM((2048, 128), f32),
            pltpu.VMEM((BUNDLE, 128), f32),
            pltpu.VMEM((512, 128), f32),
            pltpu.SemaphoreType.DMA((14,)),
        ],
    )(
        device,
        leaf_order,
        near_lists.T,
        points,
        right_sides,
        leaf_basis,
        transfer_low,
        transfer_top,
        proxy_low,
    )
    near_2 = swap(pack, 0, 1, 256)
    near_3 = swap(pack, 1, 1, 256)
    near_0 = swap(pack, 0, 16, 256)
    near_1 = swap(pack, 1, 16, 256)

    scratch = [
        pltpu.VMEM((2080, 128), f32),
        pltpu.VMEM((UNROLL, 256, 128), f32),
        pltpu.VMEM((UNROLL, 256, 128), bf16),
        pltpu.SMEM((LIST,), jnp.int32),
    ]
    near = None
    begin = 0
    for count in LOCAL_PARTS:

        def body(*refs, begin=begin, count=count):
            local_kernel(begin, count, *refs)

        operands = (tasks, pack) + ((near,) if begin else ())
        begin += count
        near = call(
            body,
            shape(2048, 128),
            [HBM] + [VMEM] * (len(operands) - 1),
            VMEM,
            3 * MICRO,
            12,
            scratch + [pltpu.VMEM((128, 128), f32), pltpu.SemaphoreType.DMA((1,))],
        )(*operands)

    low_part = call(
        far_kernel,
        shape(512, 32),
        [SMEM] + [HBM] * 4,
        VMEM,
        4 * MICRO,
        12,
        [
            pltpu.SMEM((16, FAR), jnp.int32),
            pltpu.VMEM((3, 144, 128), f32),
            pltpu.SemaphoreType.DMA((4,)),
        ],
    )(device, far_lists, near_2, pack, near_3)

    partials = slice(HALO_AT + 128, HALO_AT + 136)
    gathered = (pack[partials] + near_2[partials]).reshape(1, 8, 128)
    for number in range(3):
        other = chip_swap(gathered, 1 << number)
        gathered = jnp.concatenate([gathered, other], axis=0)
    pieces = [gathered]
    for by in range(1, 4):
        pieces.append(chip_swap(gathered, 8 * by))
    gathered = jnp.concatenate(pieces, axis=0)
    pieces = [gathered]
    for by in range(1, 4):
        pieces.append(chip_swap(gathered, 32 * by))

    for count in REMOTE_PARTS:

        def body(*refs, begin=begin, count=count):
            remote_kernel(begin, count, *refs)

        begin += count
        near = call(
            body,
            shape(2048, 128),
            [SMEM, HBM, VMEM, HBM, HBM, HBM, HBM, VMEM],
            VMEM,
            4 * MICRO,
            24,
            scratch
            + [
                pltpu.VMEM((512, 128), f32),
                pltpu.VMEM((8192, 128), f32),
                pltpu.VMEM((512, 128), f32),
                pltpu.SMEM((64,), jnp.int32),
                pltpu.SemaphoreType.DMA((9,)),
            ],
        )(device, tasks, pack, near_0, near_1, near_2, near_3, near)

    return call(
        down_kernel,
        shape(RHS, LPD * LEAF),
        [SMEM] * 4 + [VMEM] * 9,
        VMEM,
        4 * MICRO,
        20,
        [pltpu.VMEM((128, 8, 128), f32), pltpu.VMEM((128, 64), f32)],
    )(
        device,
        leaf_order,
        top_lists,
        subtree_map,
        *pieces,
        proxy_top.transpose(1, 2, 0),
        transfer_top,
        low_part,
        weights,
        near,
    )


def solution(mesh):
    return jax.shard_map(
        product,
        mesh=mesh,
        in_specs=(
            P(None, ("leaf", "sub")),
            P(None, ("leaf", "sub")),
            P(("leaf", "sub")),
            P(("leaf", "sub"), None, None),
            P(("leaf", "sub"), None, None),
            P(("leaf", "sub"), None, None),
            P(("leaf", "sub"), None, None),
            P(),
            P(("leaf", "sub"), None),
            P(("leaf", "sub"), None),
            P("leaf", None),
            P(),
        ),
        out_specs=P(None, ("leaf", "sub")),
        check_vma=False,
    )
```

time: 122 us -> 109 us (0.89)
  the two profiles are of different devices: /device:TPU:1 before, /device:TPU:230 now
where the time goes in v1:
time: 109 us; the launch traced here: 108 us
  Pallas kernels  49.1 us (45%)
  waiting for transfers between devices  39.2 us (36%)
  starting transfers between devices  17.2 us (16%)
  local copies, waits for them, and re-layouts  2.01 us (2%)
    ppermute x9, waiting for transfers between devices, chip_swap(): return lax.ppermute(x, 'leaf', [(i, i ^ bits) for i in range(128)])  39.2 us
    pallas_call x3, Pallas kernels, product(): call(body, shape(2048, 128), [HBM] + [VMEM] * (len(operands) - 1), VMEM,...  21 us
    pallas_call x1, Pallas kernels, product(): call(body, shape(2048, 128), [SMEM, HBM, VMEM, HBM, HBM, HBM, HBM, VMEM],...  15.7 us
    ppermute x9, starting transfers between devices, chip_swap(): return lax.ppermute(x, 'leaf', [(i, i ^ bits) for i in range(128)])  9.1 us
    ppermute x4, starting transfers between devices, swap(): return lax.ppermute(x, AXES, pairs)  8.11 us
    pallas_call x1, Pallas kernels, product(): call(up_kernel, (shape(BUNDLE, 128), shape(2048, 128), shape(LIST, dtype=...  5.94 us
    pallas_call x1, Pallas kernels, product(): call(far_kernel, shape(512, 32), [SMEM] + [HBM] * 4, VMEM, 4 * MICRO, 12,...  3.46 us
    pallas_call x1, Pallas kernels, product(): call(down_kernel, shape(RHS, LPD * LEAF), [SMEM] * 4 + [VMEM] * 9, VMEM,...  3.01 us
  transfers between devices with their start and end apart: 13, of which 5 were waited for; matrix products, arithmetic and copies ran while one was open for 1% of the time, Pallas kernels for 37%

profile of v1, /device:TPU:230, one launch (start us, length us, event | category | flops | bytes accessed | tf_op | source)
XLA Modules:
  0.0 108.5 jit_solution(5538814835860428894)
XLA Ops:
  0.0 5.9 %shard_map.118 = (f32[2320,128]{1,0:T(8,128)}, f32[2048,128]{1,0:T(8,128)}, s32[640]{0:T(1024)}) custom-call(s32[1]{0:T(128)} %bitcast.device.refs_0_, s32[64]{0:T(128)} %order.1, s32[9,64]{1,0:T(8,128)} %bitcast.7, f32[2,8192]{1,0:T(2,128)} %points_in.1, f32[32,8192]{1,0:T(8,128)} %values_in.1, f32[64,32,128]{2,1,0:T(8,128)} %basis_in.1, ...), custom_call_target="tpu_custom_call" | custom-call | flops 8000000 | tf_op jit(solution)/shard_map/pallas_call | solution.py:403
  6.0 5.2 %collective-permute-start.12 = (f32[2320,128]{1,0:T(8,128)}, f32[2320,128]{1,0:T(8,128)S(1)}, u32[]{:S(2)}, u32[]{:S(2)}) collective-permute-start(f32[2320,128]{1,0:T(8,128)} %get-tuple-element.8.own_in.refs_1_.refs_2_), channel_id=1, source_target_pairs={{16,32},{32,16},{17,33},{33,17},{18,34},{34,18},{19,35},{35,19},{2... | collective-permute-start | bytes 3563528 | tf_op jit(solution)/shard_map/ppermute | solution.py:375
  11.3 2.7 %collective-permute-start.10 = (f32[2320,128]{1,0:T(8,128)}, f32[2320,128]{1,0:T(8,128)S(1)}, u32[]{:S(2)}, u32[]{:S(2)}) collective-permute-start(f32[2320,128]{1,0:T(8,128)} %get-tuple-element.8.own_in.refs_1_.refs_2_), channel_id=1, source_target_pairs={{1,2},{2,1},{3,4},{4,3},{5,6},{6,5},{7,8},{8,7},{9,10},{10,9},{11,... | collective-permute-start | bytes 3563528 | tf_op jit(solution)/shard_map/ppermute | solution.py:375
  14.1 0.7 constant_dynamic-update-slice_fusion.6
  14.8 1.0 collective-permute-start.1
  15.8 12.4 %collective-permute-done.1 = f32[1,8,128]{2,1,0:T(8,128)S(1)} collective-permute-done((f32[1,8,128]{2,1,0:T(8,128)S(1)}, f32[1,8,128]{2,1,0:T(8,128)S(1)}, u32[]{:S(2)}, u32[]{:S(2)}) %collective-permute-start.1) | collective-permute-done | bytes 4128 | tf_op jit(solution)/shard_map/ppermute | solution.py:379
  28.2 1.5 %collective-permute-start.2 = (f32[2,8,128]{2,1,0:T(8,128)S(1)}, f32[2,8,128]{2,1,0:T(8,128)S(1)}, u32[]{:S(2)}, u32[]{:S(2)}) collective-permute-start(f32[2,8,128]{2,1,0:T(8,128)S(1)} %pad_maximum_fusion.2), channel_id=1, source_target_pairs={{0,4},{2,6},{4,0},{6,2},{8,12},{10,14},{12,8},{14,10},{16,20},{18,... | collective-permute-start | bytes 24584 | tf_op jit(solution)/shard_map/ppermute | solution.py:379
  29.7 3.1 %collective-permute-done.2 = f32[2,8,128]{2,1,0:T(8,128)S(1)} collective-permute-done((f32[2,8,128]{2,1,0:T(8,128)S(1)}, f32[2,8,128]{2,1,0:T(8,128)S(1)}, u32[]{:S(2)}, u32[]{:S(2)}) %collective-permute-start.2) | collective-permute-done | bytes 8224 | tf_op jit(solution)/shard_map/ppermute | solution.py:379
  32.8 0.6 collective-permute-start.3
  33.4 7.0 %collective-permute-done.3 = f32[4,8,128]{2,1,0:T(8,128)S(1)} collective-permute-done((f32[4,8,128]{2,1,0:T(8,128)S(1)}, f32[4,8,128]{2,1,0:T(8,128)S(1)}, u32[]{:S(2)}, u32[]{:S(2)}) %collective-permute-start.3) | collective-permute-done | bytes 16416 | tf_op jit(solution)/shard_map/ppermute | solution.py:379
  40.4 0.6 collective-permute-start.6
  41.1 1.1 %collective-permute-start.4 = (f32[8,8,128]{2,1,0:T(8,128)S(1)}, f32[8,8,128]{2,1,0:T(8,128)S(1)}, u32[]{:S(2)}, u32[]{:S(2)}) collective-permute-start(f32[8,8,128]{2,1,0:T(8,128)S(1)} %pad_maximum_fusion), channel_id=1, source_target_pairs={{0,16},{2,18},{4,20},{6,22},{8,24},{10,26},{12,28},{14,30},{16,0},... | collective-permute-start | bytes 98312 | tf_op jit(solution)/shard_map/ppermute | solution.py:379
  42.2 11.3 %collective-permute-done.4 = f32[8,8,128]{2,1,0:T(8,128)S(1)} collective-permute-done((f32[8,8,128]{2,1,0:T(8,128)S(1)}, f32[8,8,128]{2,1,0:T(8,128)S(1)}, u32[]{:S(2)}, u32[]{:S(2)}) %collective-permute-start.4) | collective-permute-done | bytes 32800 | tf_op jit(solution)/shard_map/ppermute | solution.py:379
  53.6 5.3 %collective-permute-done.5 = f32[8,8,128]{2,1,0:T(8,128)S(1)} collective-permute-done((f32[8,8,128]{2,1,0:T(8,128)S(1)}, f32[8,8,128]{2,1,0:T(8,128)S(1)}, u32[]{:S(2)}, u32[]{:S(2)}) %collective-permute-start.5) | collective-permute-done | bytes 32800 | tf_op jit(solution)/shard_map/ppermute | solution.py:379
  59.0 2.6 %collective-permute-start.8 = (f32[32,8,128]{2,1,0:T(8,128)S(1)}, f32[32,8,128]{2,1,0:T(8,128)S(1)}, u32[]{:S(2)}, u32[]{:S(2)}) collective-permute-start(f32[32,8,128]{2,1,0:T(8,128)S(1)} %constant_dynamic-update-slice_fusion.piece_0), channel_id=1, source_target_pairs={{0,128},{2,130},{4,132},{6,134},{8,136},{10,138},{12,140},{14,142}... | collective-permute-start | bytes 393224 | tf_op jit(solution)/shard_map/ppermute | solution.py:379
  61.6 1.5 %collective-permute-start.7 = (f32[32,8,128]{2,1,0:T(8,128)S(1)}, f32[32,8,128]{2,1,0:T(8,128)S(1)}, u32[]{:S(2)}, u32[]{:S(2)}) collective-permute-start(f32[32,8,128]{2,1,0:T(8,128)S(1)} %constant_dynamic-update-slice_fusion.piece_0), channel_id=1, source_target_pairs={{0,64},{2,66},{4,68},{6,70},{8,72},{10,74},{12,76},{14,78},{16,80}... | collective-permute-start | bytes 393224 | tf_op jit(solution)/shard_map/ppermute | solution.py:379
  63.1 1.3 %copy-done = f32[2320,128]{1,0:T(8,128)S(1)} copy-done((f32[2320,128]{1,0:T(8,128)S(1)}, f32[2320,128]{1,0:T(8,128)}, u32[]{:S(2)}) %copy-start) | copy-done | bytes 1187864
  64.4 0.7 copy-done.4
  65.0 7.2 %shard_map.120.refs_2_ = f32[2048,128]{1,0:T(8,128)S(1)} custom-call(s32[640]{0:T(1024)S(1)} %copy-done.4, f32[2320,128]{1,0:T(8,128)S(1)} %copy-done), custom_call_target="tpu_custom_call" | custom-call | flops 6000000 | tf_op jit(solution)/shard_map/pallas_call | solution.py:455
  72.3 6.9 %shard_map.121.refs_2_ = f32[2048,128]{1,0:T(8,128)S(1)} custom-call(s32[640]{0:T(1024)S(1)} %copy-done.4, f32[2320,128]{1,0:T(8,128)S(1)} %copy-done, f32[2048,128]{1,0:T(8,128)S(1)} %shard_map.120.refs_2_), custom_call_target="tpu_custom_call" | custom-call | flops 6000000 | tf_op jit(solution)/shard_map/pallas_call | solution.py:455
  79.2 6.9 %shard_map.122.refs_7_ = f32[2048,128]{1,0:T(8,128)S(1)} custom-call(s32[640]{0:T(1024)S(1)} %copy-done.4, f32[2320,128]{1,0:T(8,128)S(1)} %copy-done, f32[2048,128]{1,0:T(8,128)S(1)} %shard_map.121.refs_2_), custom_call_target="tpu_custom_call" | custom-call | flops 6000000 | tf_op jit(solution)/shard_map/pallas_call | solution.py:455
  86.1 3.5 %shard_map.119.low_part = f32[512,32]{1,0:T(8,128)S(1)} custom-call(s32[1]{0:T(128)} %bitcast.device.refs_0_, s32[16,27]{1,0:T(8,128)S(1)} %copy-done.6, f32[2320,128]{1,0:T(8,128)S(1)} %collective-permute-done.beside_in.refs_5_, f32[2320,128]{1,0:T(8,128)S(1)} %copy-done.1, f32[2320,128]{1,0:T(8,128)S(1)} %collective-permute-done.10.across_in.refs_6_), custom_call_target="tpu_custom_call" | custom-call | flops 8000000 | tf_op jit(solution)/shard_map/pallas_call | solution.py:465
  89.7 15.7 %shard_map.123.near = f32[2048,128]{1,0:T(8,128)S(1)} custom-call(s32[1]{0:T(128)} %bitcast.device.refs_0_, s32[640]{0:T(1024)S(1)} %copy-done.4, f32[2320,128]{1,0:T(8,128)S(1)} %copy-done.1, f32[2320,128]{1,0:T(8,128)S(1)} %collective-permute-done.11.refs_3_, f32[2320,128]{1,0:T(8,128)S(1)} %collective-permute-done.12.refs_4_, ...), custom_call_target="tpu_custom_call" | custom-call | flops 8000000 | tf_op jit(solution)/shard_map/pallas_call | solution.py:498
  105.5 3.0 %shard_map.124 = f32[32,8192]{1,0:T(8,128)} custom-call(s32[1]{0:T(128)} %bitcast.device.refs_0_, s32[64]{0:T(128)S(1)} %copy-done.7, s32[1,27]{1,0:T(1,128)S(1)} %copy-done.8, s32[128]{0:T(128)S(1)} %copy-done.9, f32[32,8,128]{2,1,0:T(8,128)S(1)} %constant_dynamic-update-slice_fusion.piece_0, f32[32,8,128]{2,1,0:T(8,128)S(1)} %collective-permute-done.7.piece_1, ...), custom_call_target="tpu_custom_call" | custom-call | flops 8000000 | tf_op jit(solution)/shard_map/pallas_call | solution.py:515
  (39 shorter events, 0.5 us)
Async XLA Ops:
  6.0 8.1 %collective-permute-start = (f32[2320,128]{1,0:T(8,128)}, f32[2320,128]{1,0:T(8,128)S(1)}, u32[]{:S(2)}, u32[]{:S(2)}) collective-permute-start(f32[2320,128]{1,0:T(8,128)} %get-tuple-element.8.own_in.refs_1_.refs_2_), channel_id=1, source_target_pairs={{0,1},{1,0},{2,3},{3,2},{4,5},{5,4},{6,7},{7,6},{8,9},{9,8},{10,11... | collective-permute-start | bytes 3563528 | tf_op jit(solution)/shard_map/ppermute | solution.py:375
  6.0 83.6 %collective-permute-start.12 = (f32[2320,128]{1,0:T(8,128)}, f32[2320,128]{1,0:T(8,128)S(1)}, u32[]{:S(2)}, u32[]{:S(2)}) collective-permute-start(f32[2320,128]{1,0:T(8,128)} %get-tuple-element.8.own_in.refs_1_.refs_2_), channel_id=1, source_target_pairs={{16,32},{32,16},{17,33},{33,17},{18,34},{34,18},{19,35},{35,19},{2... | collective-permute-start | bytes 3563528 | tf_op jit(solution)/shard_map/ppermute | solution.py:375
  11.2 78.4 %collective-permute-start.11 = (f32[2320,128]{1,0:T(8,128)}, f32[2320,128]{1,0:T(8,128)S(1)}, u32[]{:S(2)}, u32[]{:S(2)}) collective-permute-start(f32[2320,128]{1,0:T(8,128)} %get-tuple-element.8.own_in.refs_1_.refs_2_), channel_id=1, source_target_pairs={{0,16},{16,0},{1,17},{17,1},{2,18},{18,2},{3,19},{19,3},{4,20},{20... | collective-permute-start | bytes 3563528 | tf_op jit(solution)/shard_map/ppermute | solution.py:375
  11.3 50.3 %collective-permute-start.10 = (f32[2320,128]{1,0:T(8,128)}, f32[2320,128]{1,0:T(8,128)S(1)}, u32[]{:S(2)}, u32[]{:S(2)}) collective-permute-start(f32[2320,128]{1,0:T(8,128)} %get-tuple-element.8.own_in.refs_1_.refs_2_), channel_id=1, source_target_pairs={{1,2},{2,1},{3,4},{4,3},{5,6},{6,5},{7,8},{8,7},{9,10},{10,9},{11,... | collective-permute-start | bytes 3563528 | tf_op jit(solution)/shard_map/ppermute | solution.py:375
  14.8 13.4 %collective-permute-start.1 = (f32[1,8,128]{2,1,0:T(8,128)S(1)}, f32[1,8,128]{2,1,0:T(8,128)S(1)}, u32[]{:S(2)}, u32[]{:S(2)}) collective-permute-start(f32[1,8,128]{2,1,0:T(8,128)S(1)} %get-tuple-element.12), channel_id=1, source_target_pairs={{0,2},{2,0},{4,6},{6,4},{8,10},{10,8},{12,14},{14,12},{16,18},{18,... | collective-permute-start | bytes 12296 | tf_op jit(solution)/shard_map/ppermute | solution.py:379
  28.2 4.5 %collective-permute-start.2 = (f32[2,8,128]{2,1,0:T(8,128)S(1)}, f32[2,8,128]{2,1,0:T(8,128)S(1)}, u32[]{:S(2)}, u32[]{:S(2)}) collective-permute-start(f32[2,8,128]{2,1,0:T(8,128)S(1)} %pad_maximum_fusion.2), channel_id=1, source_target_pairs={{0,4},{2,6},{4,0},{6,2},{8,12},{10,14},{12,8},{14,10},{16,20},{18,... | collective-permute-start | bytes 24584 | tf_op jit(solution)/shard_map/ppermute | solution.py:379
  32.8 7.6 %collective-permute-start.3 = (f32[4,8,128]{2,1,0:T(8,128)S(1)}, f32[4,8,128]{2,1,0:T(8,128)S(1)}, u32[]{:S(2)}, u32[]{:S(2)}) collective-permute-start(f32[4,8,128]{2,1,0:T(8,128)S(1)} %pad_maximum_fusion.1), channel_id=1, source_target_pairs={{0,8},{2,10},{4,12},{6,14},{8,0},{10,2},{12,4},{14,6},{16,24},{18,... | collective-permute-start | bytes 49160 | tf_op jit(solution)/shard_map/ppermute | solution.py:379
  40.4 18.5 %collective-permute-start.6 = (f32[8,8,128]{2,1,0:T(8,128)S(1)}, f32[8,8,128]{2,1,0:T(8,128)S(1)}, u32[]{:S(2)}, u32[]{:S(2)}) collective-permute-start(f32[8,8,128]{2,1,0:T(8,128)S(1)} %pad_maximum_fusion), channel_id=1, source_target_pairs={{0,48},{2,50},{4,52},{6,54},{8,56},{10,58},{12,60},{14,62},{16,32}... | collective-permute-start | bytes 98312 | tf_op jit(solution)/shard_map/ppermute | solution.py:379
  41.1 12.4 %collective-permute-start.4 = (f32[8,8,128]{2,1,0:T(8,128)S(1)}, f32[8,8,128]{2,1,0:T(8,128)S(1)}, u32[]{:S(2)}, u32[]{:S(2)}) collective-permute-start(f32[8,8,128]{2,1,0:T(8,128)S(1)} %pad_maximum_fusion), channel_id=1, source_target_pairs={{0,16},{2,18},{4,20},{6,22},{8,24},{10,26},{12,28},{14,30},{16,0},... | collective-permute-start | bytes 98312 | tf_op jit(solution)/shard_map/ppermute | solution.py:379
  53.5 5.4 %collective-permute-start.5 = (f32[8,8,128]{2,1,0:T(8,128)S(1)}, f32[8,8,128]{2,1,0:T(8,128)S(1)}, u32[]{:S(2)}, u32[]{:S(2)}) collective-permute-start(f32[8,8,128]{2,1,0:T(8,128)S(1)} %pad_maximum_fusion), channel_id=1, source_target_pairs={{0,32},{2,34},{4,36},{6,38},{8,40},{10,42},{12,44},{14,46},{16,48}... | collective-permute-start | bytes 98312 | tf_op jit(solution)/shard_map/ppermute | solution.py:379
  58.9 46.5 %collective-permute-start.9 = (f32[32,8,128]{2,1,0:T(8,128)S(1)}, f32[32,8,128]{2,1,0:T(8,128)S(1)}, u32[]{:S(2)}, u32[]{:S(2)}) collective-permute-start(f32[32,8,128]{2,1,0:T(8,128)S(1)} %constant_dynamic-update-slice_fusion.piece_0), channel_id=1, source_target_pairs={{0,192},{2,194},{4,196},{6,198},{8,200},{10,202},{12,204},{14,206}... | collective-permute-start | bytes 393224 | tf_op jit(solution)/shard_map/ppermute | solution.py:379
  59.0 46.4 %collective-permute-start.8 = (f32[32,8,128]{2,1,0:T(8,128)S(1)}, f32[32,8,128]{2,1,0:T(8,128)S(1)}, u32[]{:S(2)}, u32[]{:S(2)}) collective-permute-start(f32[32,8,128]{2,1,0:T(8,128)S(1)} %constant_dynamic-update-slice_fusion.piece_0), channel_id=1, source_target_pairs={{0,128},{2,130},{4,132},{6,134},{8,136},{10,138},{12,140},{14,142}... | collective-permute-start | bytes 393224 | tf_op jit(solution)/shard_map/ppermute | solution.py:379
  61.6 43.8 %collective-permute-start.7 = (f32[32,8,128]{2,1,0:T(8,128)S(1)}, f32[32,8,128]{2,1,0:T(8,128)S(1)}, u32[]{:S(2)}, u32[]{:S(2)}) collective-permute-start(f32[32,8,128]{2,1,0:T(8,128)S(1)} %constant_dynamic-update-slice_fusion.piece_0), channel_id=1, source_target_pairs={{0,64},{2,66},{4,68},{6,70},{8,72},{10,74},{12,76},{14,78},{16,80}... | collective-permute-start | bytes 393224 | tf_op jit(solution)/shard_map/ppermute | solution.py:379
  63.1 1.3 %copy-start = (f32[2320,128]{1,0:T(8,128)S(1)}, f32[2320,128]{1,0:T(8,128)}, u32[]{:S(2)}) copy-start(f32[2320,128]{1,0:T(8,128)} %get-tuple-element.8.own_in.refs_1_.refs_2_) | copy-start | bytes 3563524
  64.4 0.7 copy-start.4
  79.2 6.9 %copy-start.1 = (f32[2320,128]{1,0:T(8,128)S(1)}, f32[2320,128]{1,0:T(8,128)}, u32[]{:S(2)}) copy-start(f32[2320,128]{1,0:T(8,128)} %get-tuple-element.8.own_in.refs_1_.refs_2_) | copy-start | bytes 3563524
  79.2 6.9 %copy-start.6 = (s32[16,27]{1,0:T(8,128)S(1)}, s32[16,27]{1,0:T(8,128)}, u32[]{:S(2)}) copy-start(s32[16,27]{1,0:T(8,128)} %far_in.1) | copy-start | bytes 5188
  89.6 15.9 %copy-start.2 = (f32[2048,128]{1,0:T(8,128)S(1)}, f32[2048,128]{1,0:T(8,128)}, u32[]{:S(2)}) copy-start(f32[2048,128]{1,0:T(8,128)} %get-tuple-element.9.weights) | copy-start | bytes 3145732
  89.6 15.9 %copy-start.3 = (f32[16,32,32]{2,1,0:T(8,128)S(1)}, f32[16,32,32]{2,1,0:T(8,128)}, u32[]{:S(2)}) copy-start(f32[16,32,32]{2,1,0:T(8,128)} %top.1) | copy-start | bytes 196612
  89.6 15.9 %copy-start.5 = (f32[128,2,32]{0,2,1:T(8,128)S(1)}, f32[128,2,32]{0,2,1:T(8,128)}, u32[]{:S(2)}) copy-start(f32[128,2,32]{0,2,1:T(8,128)} %param.19) | copy-start | bytes 98308
  89.6 15.9 %copy-start.7 = (s32[64]{0:T(128)S(1)}, s32[64]{0:T(128)}, u32[]{:S(2)}) copy-start(s32[64]{0:T(128)} %order.1) | copy-start | bytes 772
  89.6 15.9 %copy-start.8 = (s32[1,27]{1,0:T(1,128)S(1)}, s32[1,27]{1,0:T(1,128)}, u32[]{:S(2)}) copy-start(s32[1,27]{1,0:T(1,128)} %top_list.1) | copy-start | bytes 328
  89.6 15.9 %copy-start.9 = (s32[128]{0:T(128)S(1)}, s32[128]{0:T(128)}, u32[]{:S(2)}) copy-start(s32[128]{0:T(128)} %chip_map.1) | copy-start | bytes 1540

commit v2 on v1

--- a/solution.py
+++ b/solution.py
@@ -14,7 +14,8 @@
 NEAR = 9
 FAR = 27
 LOCAL = LPD * NEAR - 256
-UNROLL = 8
+NEAR_UNROLL = 8
+FAR_UNROLL = 16
 UP_UNROLL = 4
 HALO_AT = 2176
 BUNDLE = HALO_AT + 144
@@ -181,21 +182,22 @@
     publish(HALO_AT, 144, 1).wait()
 
 
-def near_run(tasks, begin, count, place, columns, table, target, acc, spread, blocks):
+def near_run(tasks, begin, count, place, columns, table, target, acc, spread, blocks, ready=()):
+    group = spread.shape[0]
+    trips = count // group
+
     def decode(trip, u):
-        index = trip * UNROLL + u
-        task = tasks[begin + jnp.clip(index, 0, count - 1)]
-        leaf = jnp.where((index >= 0) & (index < count), task >> 12, LPD)
-        return leaf, task >> 12, place((task >> 6) & 63), task & (LPD - 1)
+        task = tasks[begin + trip * group + u]
+        return task >> 12, place((task >> 6) & 63), task & (LPD - 1)
 
     def widen(trip, u):
-        _, _, slot, source = decode(trip, u)
+        _, slot, source = decode(trip, u)
         points = columns[pl.ds(pl.multiple_of(slot * 128, 128), 128), :]
         spread[u, 0:128, :] = lanes(points, 2 * source)
         spread[u, 128:256, :] = lanes(points, 2 * source + 1)
 
     def make(trip, u):
-        _, leaf, _, _ = decode(trip, u)
+        leaf, _, _ = decode(trip, u)
         row_x = target[pl.ds(2048 + 2 * leaf, 1), :]
         row_y = target[pl.ds(2049 + 2 * leaf, 1), :]
         kernel = decay(spread[u, 0:128, :] - row_x, spread[u, 128:256, :] - row_y)
@@ -204,7 +206,7 @@
         blocks[u, 128:256, :] = low
 
     def multiply(trip, u):
-        leaf, _, slot, source = decode(trip, u)
+        leaf, slot, source = decode(trip, u)
         at = pl.multiple_of(slot * 2048 + 32 * source, 32)
         high, low = split(table[pl.ds(at, 32), :])
         left = jnp.concatenate(
@@ -219,13 +221,29 @@
         acc[rows, :] += result[0:32] + result[32:64]
 
     def step(trip, carry):
-        for u in range(UNROLL):
+        for u in range(group):
             multiply(trip - 2, u)
+        for u in range(group):
             make(trip - 1, u)
+        for u in range(group):
             widen(trip, u)
         return carry
 
-    lax.fori_loop(0, count // UNROLL + 2, step, 0)
+    for u in range(group):
+        widen(0, u)
+    for u in range(group):
+        make(0, u)
+    for u in range(group):
+        widen(1, u)
+    for copy in ready:
+        copy.wait()
+    lax.fori_loop(2, trips, step, 0)
+    for u in range(group):
+        multiply(trips - 2, u)
+    for u in range(group):
+        make(trips - 1, u)
+    for u in range(group):
+        multiply(trips - 1, u)
 
 
 def local_kernel(begin, count, *refs):
@@ -233,11 +251,11 @@
     before = refs[2] if begin else None
     out, acc, spread, blocks, tasks, columns, semaphores = refs[-7:]
     (copy,) = fetch([(tasks_in, tasks)], semaphores)
-    acc[0:2048, :] = before[...] if begin else jnp.zeros((2048, 128), f32)
+    acc[...] = before[...] if begin else jnp.zeros((2048, 128), f32)
     columns[...] = pack[2048:2176, :].T
     copy.wait()
     near_run(tasks, begin, count, lambda code: 0, columns, pack, pack, acc, spread, blocks)
-    out[...] = acc[0:2048, :]
+    out[...] = acc[...]
 
 
 def remote_kernel(begin, count, device, tasks_in, pack, near_0, near_1, near_2, near_3, before, *refs):
@@ -248,7 +266,7 @@
         pairs.append((fetched[number].at[pl.ds(2048, 128)], points.at[pl.ds(128 * number, 128)]))
         pairs.append((fetched[number].at[pl.ds(0, 2048)], table.at[pl.ds(2048 * number, 2048)]))
     copies = fetch(pairs, semaphores)
-    acc[0:2048, :] = before[...]
+    acc[...] = before[...]
     row, column = (device[0] >> 4) & 1, device[0] & 1
     slots[0], slots[32] = 1 - row, row
     slots[15], slots[17] = 3 - column, 2 + column
@@ -258,12 +276,20 @@
         columns[128 * number : 128 * number + 128, :] = points[
             128 * number : 128 * number + 128, :
         ].T
-    for number in range(4):
-        copies[2 * number + 2].wait()
     near_run(
-        tasks, begin, count, lambda code: slots[code], columns, table, pack, acc, spread, blocks
-    )
-    out[...] = acc[0:2048, :]
+        tasks,
+        begin,
+        count,
+        lambda code: slots[code],
+        columns,
+        table,
+        pack,
+        acc,
+        spread,
+        blocks,
+        [copies[2 * number + 2] for number in range(4)],
+    )
+    out[...] = acc[...]
 
 
 def far_kernel(device, far_in, beside_in, own_in, across_in, out, far, halos, semaphores):
@@ -308,11 +334,14 @@
 
 
 def down_kernel(
-    device, order, top_list, chip_map, piece_0, piece_1, piece_2, piece_3, proxy_top, top, low_part, weights, near, out, gathered, turned
+    device, order_in, list_in, map_in, piece_0, piece_1, piece_2, piece_3, proxy_top, top, low_part, weights, near, out, gathered, turned, order, top_list, chip_map, semaphores
 ):
+    copies = fetch(((list_in, top_list), (map_in, chip_map), (order_in, order)), semaphores)
     for number, piece in enumerate((piece_0, piece_1, piece_2, piece_3)):
         gathered[32 * number : 32 * number + 32] = piece[...]
     turned[...] = proxy_top[...].reshape(64, 128).T
+    for copy in copies:
+        copy.wait()
     chip = device[0] // 2
     t_x = lanes(proxy_top[0], chip)
     t_y = lanes(proxy_top[1], chip)
@@ -437,12 +466,14 @@
     near_0 = swap(pack, 0, 16, 256)
     near_1 = swap(pack, 1, 16, 256)
 
-    scratch = [
-        pltpu.VMEM((2080, 128), f32),
-        pltpu.VMEM((UNROLL, 256, 128), f32),
-        pltpu.VMEM((UNROLL, 256, 128), bf16),
-        pltpu.SMEM((LIST,), jnp.int32),
-    ]
+    def scratch(group):
+        return [
+            pltpu.VMEM((2048, 128), f32),
+            pltpu.VMEM((group, 256, 128), f32),
+            pltpu.VMEM((group, 256, 128), bf16),
+            pltpu.SMEM((LIST,), jnp.int32),
+        ]
+
     near = None
     begin = 0
     for count in LOCAL_PARTS:
@@ -459,7 +490,7 @@
             VMEM,
             3 * MICRO,
             12,
-            scratch + [pltpu.VMEM((128, 128), f32), pltpu.SemaphoreType.DMA((1,))],
+            scratch(NEAR_UNROLL) + [pltpu.VMEM((128, 128), f32), pltpu.SemaphoreType.DMA((1,))],
         )(*operands)
 
     low_part = call(
@@ -502,7 +533,7 @@
             VMEM,
             4 * MICRO,
             24,
-            scratch
+            scratch(FAR_UNROLL)
             + [
                 pltpu.VMEM((512, 128), f32),
                 pltpu.VMEM((8192, 128), f32),
@@ -515,11 +546,18 @@
     return call(
         down_kernel,
         shape(RHS, LPD * LEAF),
-        [SMEM] * 4 + [VMEM] * 9,
+        [SMEM] + [HBM] * 3 + [VMEM] * 9,
         VMEM,
         4 * MICRO,
         20,
-        [pltpu.VMEM((128, 8, 128), f32), pltpu.VMEM((128, 64), f32)],
+        [
+            pltpu.VMEM((128, 8, 128), f32),
+            pltpu.VMEM((128, 64), f32),
+            pltpu.SMEM((LPD,), jnp.int32),
+            pltpu.SMEM((1, FAR), jnp.int32),
+            pltpu.SMEM((128,), jnp.int32),
+            pltpu.SemaphoreType.DMA((3,)),
+        ],
     )(
         device,
         leaf_order,

time: 109 us -> 106 us (0.972)
  Pallas kernels: 49.1 us -> 46.5 us
    pallas_call x1, Pallas kernels: 15.7 us -> 14 us  [product(): call(body, shape(2048, 128), [SMEM, HBM, VMEM, HBM, HBM, HBM, HBM, VMEM],...]
  transfers between devices with their start and end apart: 13 -> 13, of which waited for: 5 -> 5; matrix products, arithmetic and copies ran while one was open for 1% -> 1% of each run, Pallas kernels for 37% -> 35%
where the time goes in v2:
time: 106 us
  Pallas kernels  46.5 us (44%)
  waiting for transfers between devices  39.2 us (37%)
  starting transfers between devices  17.2 us (16%)
  local copies, waits for them, and re-layouts  2.01 us (2%)
    ppermute x9, waiting for transfers between devices, chip_swap(): return lax.ppermute(x, 'leaf', [(i, i ^ bits) for i in range(128)])  39.2 us
    pallas_call x3, Pallas kernels, product(): call(body, shape(2048, 128), [HBM] + [VMEM] * (len(operands) - 1), VMEM,...  20.2 us
    pallas_call x1, Pallas kernels, product(): call(body, shape(2048, 128), [SMEM, HBM, VMEM, HBM, HBM, HBM, HBM, VMEM],...  14 us
    ppermute x9, starting transfers between devices, chip_swap(): return lax.ppermute(x, 'leaf', [(i, i ^ bits) for i in range(128)])  9.1 us
    ppermute x4, starting transfers between devices, swap(): return lax.ppermute(x, AXES, pairs)  8.11 us
    pallas_call x1, Pallas kernels, product(): call(up_kernel, (shape(BUNDLE, 128), shape(2048, 128), shape(LIST, dtype=...  5.94 us
    pallas_call x1, Pallas kernels, product(): call(far_kernel, shape(512, 32), [SMEM] + [HBM] * 4, VMEM, 4 * MICRO, 12,...  3.46 us
    pallas_call x1, Pallas kernels, product(): call(down_kernel, shape(RHS, LPD * LEAF), [SMEM] + [HBM] * 3 + [VMEM] * 9...  2.94 us
  transfers between devices with their start and end apart: 13, of which 5 were waited for; matrix products, arithmetic and copies ran while one was open for 1% of the time, Pallas kernels for 35%

profile of v2, /device:TPU:230, one launch (start us, length us, event | category | flops | bytes accessed | tf_op | source)
XLA Modules:
  0.0 106.1 jit_solution(17809170145257039286)
XLA Ops:
  0.0 5.9 %shard_map.118 = (f32[2320,128]{1,0:T(8,128)}, f32[2048,128]{1,0:T(8,128)}, s32[640]{0:T(1024)}) custom-call(s32[1]{0:T(128)} %bitcast.device.refs_0_, s32[64]{0:T(128)} %order_in.3, s32[9,64]{1,0:T(8,128)} %bitcast.7, f32[2,8192]{1,0:T(2,128)} %points_in.1, f32[32,8192]{1,0:T(8,128)} %values_in.1, f32[64,32,128]{2,1,0:T(8,128)} %basis_in.1, ...), custom_call_target="tpu_custom_call" | custom-call | flops 8000000 | tf_op jit(solution)/shard_map/pallas_call | solution.py:432
  6.0 5.2 %collective-permute-start.12 = (f32[2320,128]{1,0:T(8,128)}, f32[2320,128]{1,0:T(8,128)S(1)}, u32[]{:S(2)}, u32[]{:S(2)}) collective-permute-start(f32[2320,128]{1,0:T(8,128)} %get-tuple-element.8.own_in.refs_1_.refs_2_), channel_id=1, source_target_pairs={{16,32},{32,16},{17,33},{33,17},{18,34},{34,18},{19,35},{35,19},{2... | collective-permute-start | bytes 3563528 | tf_op jit(solution)/shard_map/ppermute | solution.py:404
  11.3 2.7 %collective-permute-start.10 = (f32[2320,128]{1,0:T(8,128)}, f32[2320,128]{1,0:T(8,128)S(1)}, u32[]{:S(2)}, u32[]{:S(2)}) collective-permute-start(f32[2320,128]{1,0:T(8,128)} %get-tuple-element.8.own_in.refs_1_.refs_2_), channel_id=1, source_target_pairs={{1,2},{2,1},{3,4},{4,3},{5,6},{6,5},{7,8},{8,7},{9,10},{10,9},{11,... | collective-permute-start | bytes 3563528 | tf_op jit(solution)/shard_map/ppermute | solution.py:404
  14.1 0.7 constant_dynamic-update-slice_fusion.6
  14.8 1.0 collective-permute-start.1
  15.8 12.4 %collective-permute-done.1 = f32[1,8,128]{2,1,0:T(8,128)S(1)} collective-permute-done((f32[1,8,128]{2,1,0:T(8,128)S(1)}, f32[1,8,128]{2,1,0:T(8,128)S(1)}, u32[]{:S(2)}, u32[]{:S(2)}) %collective-permute-start.1) | collective-permute-done | bytes 4128 | tf_op jit(solution)/shard_map/ppermute | solution.py:408
  28.2 1.5 %collective-permute-start.2 = (f32[2,8,128]{2,1,0:T(8,128)S(1)}, f32[2,8,128]{2,1,0:T(8,128)S(1)}, u32[]{:S(2)}, u32[]{:S(2)}) collective-permute-start(f32[2,8,128]{2,1,0:T(8,128)S(1)} %pad_maximum_fusion.2), channel_id=1, source_target_pairs={{0,4},{2,6},{4,0},{6,2},{8,12},{10,14},{12,8},{14,10},{16,20},{18,... | collective-permute-start | bytes 24584 | tf_op jit(solution)/shard_map/ppermute | solution.py:408
  29.7 3.1 %collective-permute-done.2 = f32[2,8,128]{2,1,0:T(8,128)S(1)} collective-permute-done((f32[2,8,128]{2,1,0:T(8,128)S(1)}, f32[2,8,128]{2,1,0:T(8,128)S(1)}, u32[]{:S(2)}, u32[]{:S(2)}) %collective-permute-start.2) | collective-permute-done | bytes 8224 | tf_op jit(solution)/shard_map/ppermute | solution.py:408
  32.8 0.6 collective-permute-start.3
  33.4 7.0 %collective-permute-done.3 = f32[4,8,128]{2,1,0:T(8,128)S(1)} collective-permute-done((f32[4,8,128]{2,1,0:T(8,128)S(1)}, f32[4,8,128]{2,1,0:T(8,128)S(1)}, u32[]{:S(2)}, u32[]{:S(2)}) %collective-permute-start.3) | collective-permute-done | bytes 16416 | tf_op jit(solution)/shard_map/ppermute | solution.py:408
  40.4 0.6 collective-permute-start.6
  41.1 1.1 %collective-permute-start.4 = (f32[8,8,128]{2,1,0:T(8,128)S(1)}, f32[8,8,128]{2,1,0:T(8,128)S(1)}, u32[]{:S(2)}, u32[]{:S(2)}) collective-permute-start(f32[8,8,128]{2,1,0:T(8,128)S(1)} %pad_maximum_fusion), channel_id=1, source_target_pairs={{0,16},{2,18},{4,20},{6,22},{8,24},{10,26},{12,28},{14,30},{16,0},... | collective-permute-start | bytes 98312 | tf_op jit(solution)/shard_map/ppermute | solution.py:408
  42.2 11.3 %collective-permute-done.4 = f32[8,8,128]{2,1,0:T(8,128)S(1)} collective-permute-done((f32[8,8,128]{2,1,0:T(8,128)S(1)}, f32[8,8,128]{2,1,0:T(8,128)S(1)}, u32[]{:S(2)}, u32[]{:S(2)}) %collective-permute-start.4) | collective-permute-done | bytes 32800 | tf_op jit(solution)/shard_map/ppermute | solution.py:408
  53.6 5.3 %collective-permute-done.5 = f32[8,8,128]{2,1,0:T(8,128)S(1)} collective-permute-done((f32[8,8,128]{2,1,0:T(8,128)S(1)}, f32[8,8,128]{2,1,0:T(8,128)S(1)}, u32[]{:S(2)}, u32[]{:S(2)}) %collective-permute-start.5) | collective-permute-done | bytes 32800 | tf_op jit(solution)/shard_map/ppermute | solution.py:408
  59.0 2.6 %collective-permute-start.8 = (f32[32,8,128]{2,1,0:T(8,128)S(1)}, f32[32,8,128]{2,1,0:T(8,128)S(1)}, u32[]{:S(2)}, u32[]{:S(2)}) collective-permute-start(f32[32,8,128]{2,1,0:T(8,128)S(1)} %constant_dynamic-update-slice_fusion.piece_0), channel_id=1, source_target_pairs={{0,128},{2,130},{4,132},{6,134},{8,136},{10,138},{12,140},{14,142}... | collective-permute-start | bytes 393224 | tf_op jit(solution)/shard_map/ppermute | solution.py:408
  61.6 1.5 %collective-permute-start.7 = (f32[32,8,128]{2,1,0:T(8,128)S(1)}, f32[32,8,128]{2,1,0:T(8,128)S(1)}, u32[]{:S(2)}, u32[]{:S(2)}) collective-permute-start(f32[32,8,128]{2,1,0:T(8,128)S(1)} %constant_dynamic-update-slice_fusion.piece_0), channel_id=1, source_target_pairs={{0,64},{2,66},{4,68},{6,70},{8,72},{10,74},{12,76},{14,78},{16,80}... | collective-permute-start | bytes 393224 | tf_op jit(solution)/shard_map/ppermute | solution.py:408
  63.1 1.3 %copy-done = f32[2320,128]{1,0:T(8,128)S(1)} copy-done((f32[2320,128]{1,0:T(8,128)S(1)}, f32[2320,128]{1,0:T(8,128)}, u32[]{:S(2)}) %copy-start) | copy-done | bytes 1187864
  64.4 0.7 copy-done.4
  65.0 7.0 %shard_map.120.refs_2_ = f32[2048,128]{1,0:T(8,128)S(1)} custom-call(s32[640]{0:T(1024)S(1)} %copy-done.4, f32[2320,128]{1,0:T(8,128)S(1)} %copy-done), custom_call_target="tpu_custom_call" | custom-call | flops 6000000 | tf_op jit(solution)/shard_map/pallas_call | solution.py:486
  72.1 6.6 %shard_map.121.refs_2_ = f32[2048,128]{1,0:T(8,128)S(1)} custom-call(s32[640]{0:T(1024)S(1)} %copy-done.4, f32[2320,128]{1,0:T(8,128)S(1)} %copy-done, f32[2048,128]{1,0:T(8,128)S(1)} %shard_map.120.refs_2_), custom_call_target="tpu_custom_call" | custom-call | flops 6000000 | tf_op jit(solution)/shard_map/pallas_call | solution.py:486
  78.7 6.6 %shard_map.122.refs_7_ = f32[2048,128]{1,0:T(8,128)S(1)} custom-call(s32[640]{0:T(1024)S(1)} %copy-done.4, f32[2320,128]{1,0:T(8,128)S(1)} %copy-done, f32[2048,128]{1,0:T(8,128)S(1)} %shard_map.121.refs_2_), custom_call_target="tpu_custom_call" | custom-call | flops 6000000 | tf_op jit(solution)/shard_map/pallas_call | solution.py:486
  85.3 3.5 %shard_map.119.low_part = f32[512,32]{1,0:T(8,128)S(1)} custom-call(s32[1]{0:T(128)} %bitcast.device.refs_0_, s32[16,27]{1,0:T(8,128)S(1)} %copy-done.6, f32[2320,128]{1,0:T(8,128)S(1)} %collective-permute-done.beside_in.refs_5_, f32[2320,128]{1,0:T(8,128)S(1)} %copy-done.1, f32[2320,128]{1,0:T(8,128)S(1)} %collective-permute-done.10.across_in.refs_6_), custom_call_target="tpu_custom_call" | custom-call | flops 8000000 | tf_op jit(solution)/shard_map/pallas_call | solution.py:496
  88.9 14.0 %shard_map.123.near = f32[2048,128]{1,0:T(8,128)S(1)} custom-call(s32[1]{0:T(128)} %bitcast.device.refs_0_, s32[640]{0:T(1024)S(1)} %copy-done.4, f32[2320,128]{1,0:T(8,128)S(1)} %copy-done.1, f32[2320,128]{1,0:T(8,128)S(1)} %collective-permute-done.11.refs_3_, f32[2320,128]{1,0:T(8,128)S(1)} %collective-permute-done.12.refs_4_, ...), custom_call_target="tpu_custom_call" | custom-call | flops 8000000 | tf_op jit(solution)/shard_map/pallas_call | solution.py:529
  103.0 2.9 %shard_map.124 = f32[32,8192]{1,0:T(8,128)} custom-call(s32[1]{0:T(128)} %bitcast.device.refs_0_, s32[64]{0:T(128)S(1)} %copy-done.7, s32[1,27]{1,0:T(1,128)S(1)} %copy-done.8, s32[128]{0:T(128)S(1)} %copy-done.9, f32[32,8,128]{2,1,0:T(8,128)S(1)} %constant_dynamic-update-slice_fusion.piece_0, f32[32,8,128]{2,1,0:T(8,128)S(1)} %collective-permute-done.7.piece_1, ...), custom_call_target="tpu_custom_call" | custom-call | flops 8000000 | tf_op jit(solution)/shard_map/pallas_call | solution.py:546
  (39 shorter events, 0.5 us)
Async XLA Ops:
  6.0 8.1 %collective-permute-start = (f32[2320,128]{1,0:T(8,128)}, f32[2320,128]{1,0:T(8,128)S(1)}, u32[]{:S(2)}, u32[]{:S(2)}) collective-permute-start(f32[2320,128]{1,0:T(8,128)} %get-tuple-element.8.own_in.refs_1_.refs_2_), channel_id=1, source_target_pairs={{0,1},{1,0},{2,3},{3,2},{4,5},{5,4},{6,7},{7,6},{8,9},{9,8},{10,11... | collective-permute-start | bytes 3563528 | tf_op jit(solution)/shard_map/ppermute | solution.py:404
  6.0 82.8 %collective-permute-start.12 = (f32[2320,128]{1,0:T(8,128)}, f32[2320,128]{1,0:T(8,128)S(1)}, u32[]{:S(2)}, u32[]{:S(2)}) collective-permute-start(f32[2320,128]{1,0:T(8,128)} %get-tuple-element.8.own_in.refs_1_.refs_2_), channel_id=1, source_target_pairs={{16,32},{32,16},{17,33},{33,17},{18,34},{34,18},{19,35},{35,19},{2... | collective-permute-start | bytes 3563528 | tf_op jit(solution)/shard_map/ppermute | solution.py:404
  11.2 77.6 %collective-permute-start.11 = (f32[2320,128]{1,0:T(8,128)}, f32[2320,128]{1,0:T(8,128)S(1)}, u32[]{:S(2)}, u32[]{:S(2)}) collective-permute-start(f32[2320,128]{1,0:T(8,128)} %get-tuple-element.8.own_in.refs_1_.refs_2_), channel_id=1, source_target_pairs={{0,16},{16,0},{1,17},{17,1},{2,18},{18,2},{3,19},{19,3},{4,20},{20... | collective-permute-start | bytes 3563528 | tf_op jit(solution)/shard_map/ppermute | solution.py:404
  11.3 50.3 %collective-permute-start.10 = (f32[2320,128]{1,0:T(8,128)}, f32[2320,128]{1,0:T(8,128)S(1)}, u32[]{:S(2)}, u32[]{:S(2)}) collective-permute-start(f32[2320,128]{1,0:T(8,128)} %get-tuple-element.8.own_in.refs_1_.refs_2_), channel_id=1, source_target_pairs={{1,2},{2,1},{3,4},{4,3},{5,6},{6,5},{7,8},{8,7},{9,10},{10,9},{11,... | collective-permute-start | bytes 3563528 | tf_op jit(solution)/shard_map/ppermute | solution.py:404
  14.8 13.4 %collective-permute-start.1 = (f32[1,8,128]{2,1,0:T(8,128)S(1)}, f32[1,8,128]{2,1,0:T(8,128)S(1)}, u32[]{:S(2)}, u32[]{:S(2)}) collective-permute-start(f32[1,8,128]{2,1,0:T(8,128)S(1)} %get-tuple-element.12), channel_id=1, source_target_pairs={{0,2},{2,0},{4,6},{6,4},{8,10},{10,8},{12,14},{14,12},{16,18},{18,... | collective-permute-start | bytes 12296 | tf_op jit(solution)/shard_map/ppermute | solution.py:408
  28.2 4.5 %collective-permute-start.2 = (f32[2,8,128]{2,1,0:T(8,128)S(1)}, f32[2,8,128]{2,1,0:T(8,128)S(1)}, u32[]{:S(2)}, u32[]{:S(2)}) collective-permute-start(f32[2,8,128]{2,1,0:T(8,128)S(1)} %pad_maximum_fusion.2), channel_id=1, source_target_pairs={{0,4},{2,6},{4,0},{6,2},{8,12},{10,14},{12,8},{14,10},{16,20},{18,... | collective-permute-start | bytes 24584 | tf_op jit(solution)/shard_map/ppermute | solution.py:408
  32.8 7.6 %collective-permute-start.3 = (f32[4,8,128]{2,1,0:T(8,128)S(1)}, f32[4,8,128]{2,1,0:T(8,128)S(1)}, u32[]{:S(2)}, u32[]{:S(2)}) collective-permute-start(f32[4,8,128]{2,1,0:T(8,128)S(1)} %pad_maximum_fusion.1), channel_id=1, source_target_pairs={{0,8},{2,10},{4,12},{6,14},{8,0},{10,2},{12,4},{14,6},{16,24},{18,... | collective-permute-start | bytes 49160 | tf_op jit(solution)/shard_map/ppermute | solution.py:408
  40.4 18.5 %collective-permute-start.6 = (f32[8,8,128]{2,1,0:T(8,128)S(1)}, f32[8,8,128]{2,1,0:T(8,128)S(1)}, u32[]{:S(2)}, u32[]{:S(2)}) collective-permute-start(f32[8,8,128]{2,1,0:T(8,128)S(1)} %pad_maximum_fusion), channel_id=1, source_target_pairs={{0,48},{2,50},{4,52},{6,54},{8,56},{10,58},{12,60},{14,62},{16,32}... | collective-permute-start | bytes 98312 | tf_op jit(solution)/shard_map/ppermute | solution.py:408
  41.1 12.4 %collective-permute-start.4 = (f32[8,8,128]{2,1,0:T(8,128)S(1)}, f32[8,8,128]{2,1,0:T(8,128)S(1)}, u32[]{:S(2)}, u32[]{:S(2)}) collective-permute-start(f32[8,8,128]{2,1,0:T(8,128)S(1)} %pad_maximum_fusion), channel_id=1, source_target_pairs={{0,16},{2,18},{4,20},{6,22},{8,24},{10,26},{12,28},{14,30},{16,0},... | collective-permute-start | bytes 98312 | tf_op jit(solution)/shard_map/ppermute | solution.py:408
  53.5 5.4 %collective-permute-start.5 = (f32[8,8,128]{2,1,0:T(8,128)S(1)}, f32[8,8,128]{2,1,0:T(8,128)S(1)}, u32[]{:S(2)}, u32[]{:S(2)}) collective-permute-start(f32[8,8,128]{2,1,0:T(8,128)S(1)} %pad_maximum_fusion), channel_id=1, source_target_pairs={{0,32},{2,34},{4,36},{6,38},{8,40},{10,42},{12,44},{14,46},{16,48}... | collective-permute-start | bytes 98312 | tf_op jit(solution)/shard_map/ppermute | solution.py:408
  58.9 44.0 %collective-permute-start.9 = (f32[32,8,128]{2,1,0:T(8,128)S(1)}, f32[32,8,128]{2,1,0:T(8,128)S(1)}, u32[]{:S(2)}, u32[]{:S(2)}) collective-permute-start(f32[32,8,128]{2,1,0:T(8,128)S(1)} %constant_dynamic-update-slice_fusion.piece_0), channel_id=1, source_target_pairs={{0,192},{2,194},{4,196},{6,198},{8,200},{10,202},{12,204},{14,206}... | collective-permute-start | bytes 393224 | tf_op jit(solution)/shard_map/ppermute | solution.py:408
  59.0 43.9 %collective-permute-start.8 = (f32[32,8,128]{2,1,0:T(8,128)S(1)}, f32[32,8,128]{2,1,0:T(8,128)S(1)}, u32[]{:S(2)}, u32[]{:S(2)}) collective-permute-start(f32[32,8,128]{2,1,0:T(8,128)S(1)} %constant_dynamic-update-slice_fusion.piece_0), channel_id=1, source_target_pairs={{0,128},{2,130},{4,132},{6,134},{8,136},{10,138},{12,140},{14,142}... | collective-permute-start | bytes 393224 | tf_op jit(solution)/shard_map/ppermute | solution.py:408
  61.6 41.3 %collective-permute-start.7 = (f32[32,8,128]{2,1,0:T(8,128)S(1)}, f32[32,8,128]{2,1,0:T(8,128)S(1)}, u32[]{:S(2)}, u32[]{:S(2)}) collective-permute-start(f32[32,8,128]{2,1,0:T(8,128)S(1)} %constant_dynamic-update-slice_fusion.piece_0), channel_id=1, source_target_pairs={{0,64},{2,66},{4,68},{6,70},{8,72},{10,74},{12,76},{14,78},{16,80}... | collective-permute-start | bytes 393224 | tf_op jit(solution)/shard_map/ppermute | solution.py:408
  63.1 1.3 %copy-start = (f32[2320,128]{1,0:T(8,128)S(1)}, f32[2320,128]{1,0:T(8,128)}, u32[]{:S(2)}) copy-start(f32[2320,128]{1,0:T(8,128)} %get-tuple-element.8.own_in.refs_1_.refs_2_) | copy-start | bytes 3563524
  64.4 0.7 copy-start.4
  78.7 6.6 %copy-start.1 = (f32[2320,128]{1,0:T(8,128)S(1)}, f32[2320,128]{1,0:T(8,128)}, u32[]{:S(2)}) copy-start(f32[2320,128]{1,0:T(8,128)} %get-tuple-element.8.own_in.refs_1_.refs_2_) | copy-start | bytes 3563524
  78.7 6.6 %copy-start.6 = (s32[16,27]{1,0:T(8,128)S(1)}, s32[16,27]{1,0:T(8,128)}, u32[]{:S(2)}) copy-start(s32[16,27]{1,0:T(8,128)} %far_in.1) | copy-start | bytes 5188
  88.8 14.1 %copy-start.2 = (f32[2048,128]{1,0:T(8,128)S(1)}, f32[2048,128]{1,0:T(8,128)}, u32[]{:S(2)}) copy-start(f32[2048,128]{1,0:T(8,128)} %get-tuple-element.9.weights) | copy-start | bytes 3145732
  88.8 14.1 %copy-start.3 = (f32[16,32,32]{2,1,0:T(8,128)S(1)}, f32[16,32,32]{2,1,0:T(8,128)}, u32[]{:S(2)}) copy-start(f32[16,32,32]{2,1,0:T(8,128)} %top.1) | copy-start | bytes 196612
  88.8 14.1 %copy-start.5 = (f32[128,2,32]{0,2,1:T(8,128)S(1)}, f32[128,2,32]{0,2,1:T(8,128)}, u32[]{:S(2)}) copy-start(f32[128,2,32]{0,2,1:T(8,128)} %param.19) | copy-start | bytes 98308
  88.8 14.1 %copy-start.7 = (s32[64]{0:T(128)S(1)}, s32[64]{0:T(128)}, u32[]{:S(2)}) copy-start(s32[64]{0:T(128)} %order_in.3) | copy-start | bytes 772
  88.8 14.1 %copy-start.8 = (s32[1,27]{1,0:T(1,128)S(1)}, s32[1,27]{1,0:T(1,128)}, u32[]{:S(2)}) copy-start(s32[1,27]{1,0:T(1,128)} %list_in.1) | copy-start | bytes 328
  88.8 14.1 %copy-start.9 = (s32[128]{0:T(128)S(1)}, s32[128]{0:T(128)}, u32[]{:S(2)}) copy-start(s32[128]{0:T(128)} %map_in.1) | copy-start | bytes 1540

commit v3 on v2

--- a/solution.py
+++ b/solution.py
@@ -14,7 +14,7 @@
 NEAR = 9
 FAR = 27
 LOCAL = LPD * NEAR - 256
-NEAR_UNROLL = 8
+NEAR_UNROLL = 16
 FAR_UNROLL = 16
 UP_UNROLL = 4
 HALO_AT = 2176
@@ -135,8 +135,8 @@
 
     def sort_leaf(leaf, local):
         code = leaf * 4096 + 1024 - base
-        for k in range(NEAR):
-            entry = near[k, leaf]
+        entries = [near[k, leaf] for k in range(NEAR)]
+        for k, entry in enumerate(entries):
             home = (entry >> 6) == device[0]
             where = jnp.where(home, local, (leaf * NEAR + (k + LOCAL)) - local)
             tasks[where] = entry + code
@@ -408,7 +408,7 @@
     return lax.ppermute(x, "leaf", [(i, i ^ bits) for i in range(128)])
 
 
-LOCAL_PARTS = (112, 104, 104)
+LOCAL_PARTS = (112, 112, 96)
 REMOTE_PARTS = (256,)
 MICRO = 2000000
 

time: 106 us -> 106 us (level)
  no operation moved by 1% of the time
where the time goes in v3:
time: 106 us; the launch traced here: 105 us
  Pallas kernels  45.9 us (43%)
  waiting for transfers between devices  39.2 us (37%)
  starting transfers between devices  17.2 us (16%)
  local copies, waits for them, and re-layouts  2.01 us (2%)
    ppermute x9, waiting for transfers between devices, chip_swap(): return lax.ppermute(x, 'leaf', [(i, i ^ bits) for i in range(128)])  39.2 us
    pallas_call x3, Pallas kernels, product(): call(body, shape(2048, 128), [HBM] + [VMEM] * (len(operands) - 1), VMEM,...  19.5 us
    pallas_call x1, Pallas kernels, product(): call(body, shape(2048, 128), [SMEM, HBM, VMEM, HBM, HBM, HBM, HBM, VMEM],...  14 us
    ppermute x9, starting transfers between devices, chip_swap(): return lax.ppermute(x, 'leaf', [(i, i ^ bits) for i in range(128)])  9.12 us
    ppermute x4, starting transfers between devices, swap(): return lax.ppermute(x, AXES, pairs)  8.09 us
    pallas_call x1, Pallas kernels, product(): call(up_kernel, (shape(BUNDLE, 128), shape(2048, 128), shape(LIST, dtype=...  5.99 us
    pallas_call x1, Pallas kernels, product(): call(far_kernel, shape(512, 32), [SMEM] + [HBM] * 4, VMEM, 4 * MICRO, 12,...  3.46 us
    pallas_call x1, Pallas kernels, product(): call(down_kernel, shape(RHS, LPD * LEAF), [SMEM] + [HBM] * 3 + [VMEM] * 9...  2.94 us
  transfers between devices with their start and end apart: 13, of which 5 were waited for; matrix products, arithmetic and copies ran while one was open for 1% of the time, Pallas kernels for 35%

profile of v3, /device:TPU:230, one launch (start us, length us, event | category | flops | bytes accessed | tf_op | source)
XLA Modules:
  0.0 105.4 jit_solution(1311721054189209484)
XLA Ops:
  0.0 6.0 %shard_map.118 = (f32[2320,128]{1,0:T(8,128)}, f32[2048,128]{1,0:T(8,128)}, s32[640]{0:T(1024)}) custom-call(s32[1]{0:T(128)} %bitcast.device.refs_0_, s32[64]{0:T(128)} %order_in.3, s32[9,64]{1,0:T(8,128)} %bitcast.7, f32[2,8192]{1,0:T(2,128)} %points_in.1, f32[32,8192]{1,0:T(8,128)} %values_in.1, f32[64,32,128]{2,1,0:T(8,128)} %basis_in.1, ...), custom_call_target="tpu_custom_call" | custom-call | flops 8000000 | tf_op jit(solution)/shard_map/pallas_call | solution.py:432
  6.1 5.2 %collective-permute-start.12 = (f32[2320,128]{1,0:T(8,128)}, f32[2320,128]{1,0:T(8,128)S(1)}, u32[]{:S(2)}, u32[]{:S(2)}) collective-permute-start(f32[2320,128]{1,0:T(8,128)} %get-tuple-element.8.own_in.refs_1_.refs_2_), channel_id=1, source_target_pairs={{16,32},{32,16},{17,33},{33,17},{18,34},{34,18},{19,35},{35,19},{2... | collective-permute-start | bytes 3563528 | tf_op jit(solution)/shard_map/ppermute | solution.py:404
  11.4 2.7 %collective-permute-start.10 = (f32[2320,128]{1,0:T(8,128)}, f32[2320,128]{1,0:T(8,128)S(1)}, u32[]{:S(2)}, u32[]{:S(2)}) collective-permute-start(f32[2320,128]{1,0:T(8,128)} %get-tuple-element.8.own_in.refs_1_.refs_2_), channel_id=1, source_target_pairs={{1,2},{2,1},{3,4},{4,3},{5,6},{6,5},{7,8},{8,7},{9,10},{10,9},{11,... | collective-permute-start | bytes 3563528 | tf_op jit(solution)/shard_map/ppermute | solution.py:404
  14.1 0.7 constant_dynamic-update-slice_fusion.6
  14.8 1.0 collective-permute-start.1
  15.8 12.4 %collective-permute-done.1 = f32[1,8,128]{2,1,0:T(8,128)S(1)} collective-permute-done((f32[1,8,128]{2,1,0:T(8,128)S(1)}, f32[1,8,128]{2,1,0:T(8,128)S(1)}, u32[]{:S(2)}, u32[]{:S(2)}) %collective-permute-start.1) | collective-permute-done | bytes 4128 | tf_op jit(solution)/shard_map/ppermute | solution.py:408
  28.3 1.5 %collective-permute-start.2 = (f32[2,8,128]{2,1,0:T(8,128)S(1)}, f32[2,8,128]{2,1,0:T(8,128)S(1)}, u32[]{:S(2)}, u32[]{:S(2)}) collective-permute-start(f32[2,8,128]{2,1,0:T(8,128)S(1)} %pad_maximum_fusion.2), channel_id=1, source_target_pairs={{0,4},{2,6},{4,0},{6,2},{8,12},{10,14},{12,8},{14,10},{16,20},{18,... | collective-permute-start | bytes 24584 | tf_op jit(solution)/shard_map/ppermute | solution.py:408
  29.7 3.1 %collective-permute-done.2 = f32[2,8,128]{2,1,0:T(8,128)S(1)} collective-permute-done((f32[2,8,128]{2,1,0:T(8,128)S(1)}, f32[2,8,128]{2,1,0:T(8,128)S(1)}, u32[]{:S(2)}, u32[]{:S(2)}) %collective-permute-start.2) | collective-permute-done | bytes 8224 | tf_op jit(solution)/shard_map/ppermute | solution.py:408
  32.8 0.7 collective-permute-start.3
  33.5 7.0 %collective-permute-done.3 = f32[4,8,128]{2,1,0:T(8,128)S(1)} collective-permute-done((f32[4,8,128]{2,1,0:T(8,128)S(1)}, f32[4,8,128]{2,1,0:T(8,128)S(1)}, u32[]{:S(2)}, u32[]{:S(2)}) %collective-permute-start.3) | collective-permute-done | bytes 16416 | tf_op jit(solution)/shard_map/ppermute | solution.py:408
  40.5 0.6 collective-permute-start.6
  41.1 1.1 %collective-permute-start.4 = (f32[8,8,128]{2,1,0:T(8,128)S(1)}, f32[8,8,128]{2,1,0:T(8,128)S(1)}, u32[]{:S(2)}, u32[]{:S(2)}) collective-permute-start(f32[8,8,128]{2,1,0:T(8,128)S(1)} %pad_maximum_fusion), channel_id=1, source_target_pairs={{0,16},{2,18},{4,20},{6,22},{8,24},{10,26},{12,28},{14,30},{16,0},... | collective-permute-start | bytes 98312 | tf_op jit(solution)/shard_map/ppermute | solution.py:408
  42.2 11.3 %collective-permute-done.4 = f32[8,8,128]{2,1,0:T(8,128)S(1)} collective-permute-done((f32[8,8,128]{2,1,0:T(8,128)S(1)}, f32[8,8,128]{2,1,0:T(8,128)S(1)}, u32[]{:S(2)}, u32[]{:S(2)}) %collective-permute-start.4) | collective-permute-done | bytes 32800 | tf_op jit(solution)/shard_map/ppermute | solution.py:408
  53.6 5.3 %collective-permute-done.5 = f32[8,8,128]{2,1,0:T(8,128)S(1)} collective-permute-done((f32[8,8,128]{2,1,0:T(8,128)S(1)}, f32[8,8,128]{2,1,0:T(8,128)S(1)}, u32[]{:S(2)}, u32[]{:S(2)}) %collective-permute-start.5) | collective-permute-done | bytes 32800 | tf_op jit(solution)/shard_map/ppermute | solution.py:408
  59.1 2.6 %collective-permute-start.8 = (f32[32,8,128]{2,1,0:T(8,128)S(1)}, f32[32,8,128]{2,1,0:T(8,128)S(1)}, u32[]{:S(2)}, u32[]{:S(2)}) collective-permute-start(f32[32,8,128]{2,1,0:T(8,128)S(1)} %constant_dynamic-update-slice_fusion.piece_0), channel_id=1, source_target_pairs={{0,128},{2,130},{4,132},{6,134},{8,136},{10,138},{12,140},{14,142}... | collective-permute-start | bytes 393224 | tf_op jit(solution)/shard_map/ppermute | solution.py:408
  61.7 1.5 %collective-permute-start.7 = (f32[32,8,128]{2,1,0:T(8,128)S(1)}, f32[32,8,128]{2,1,0:T(8,128)S(1)}, u32[]{:S(2)}, u32[]{:S(2)}) collective-permute-start(f32[32,8,128]{2,1,0:T(8,128)S(1)} %constant_dynamic-update-slice_fusion.piece_0), channel_id=1, source_target_pairs={{0,64},{2,66},{4,68},{6,70},{8,72},{10,74},{12,76},{14,78},{16,80}... | collective-permute-start | bytes 393224 | tf_op jit(solution)/shard_map/ppermute | solution.py:408
  63.1 1.3 %copy-done = f32[2320,128]{1,0:T(8,128)S(1)} copy-done((f32[2320,128]{1,0:T(8,128)S(1)}, f32[2320,128]{1,0:T(8,128)}, u32[]{:S(2)}) %copy-start) | copy-done | bytes 1187864
  64.4 0.7 copy-done.4
  65.1 6.9 %shard_map.120.refs_2_ = f32[2048,128]{1,0:T(8,128)S(1)} custom-call(s32[640]{0:T(1024)S(1)} %copy-done.4, f32[2320,128]{1,0:T(8,128)S(1)} %copy-done), custom_call_target="tpu_custom_call" | custom-call | flops 6000000 | tf_op jit(solution)/shard_map/pallas_call | solution.py:486
  72.0 6.7 %shard_map.121.refs_2_ = f32[2048,128]{1,0:T(8,128)S(1)} custom-call(s32[640]{0:T(1024)S(1)} %copy-done.4, f32[2320,128]{1,0:T(8,128)S(1)} %copy-done, f32[2048,128]{1,0:T(8,128)S(1)} %shard_map.120.refs_2_), custom_call_target="tpu_custom_call" | custom-call | flops 6000000 | tf_op jit(solution)/shard_map/pallas_call | solution.py:486
  78.7 5.9 %shard_map.122.refs_7_ = f32[2048,128]{1,0:T(8,128)S(1)} custom-call(s32[640]{0:T(1024)S(1)} %copy-done.4, f32[2320,128]{1,0:T(8,128)S(1)} %copy-done, f32[2048,128]{1,0:T(8,128)S(1)} %shard_map.121.refs_2_), custom_call_target="tpu_custom_call" | custom-call | flops 6000000 | tf_op jit(solution)/shard_map/pallas_call | solution.py:486
  84.7 3.5 %shard_map.119.low_part = f32[512,32]{1,0:T(8,128)S(1)} custom-call(s32[1]{0:T(128)} %bitcast.device.refs_0_, s32[16,27]{1,0:T(8,128)S(1)} %copy-done.6, f32[2320,128]{1,0:T(8,128)S(1)} %collective-permute-done.beside_in.refs_5_, f32[2320,128]{1,0:T(8,128)S(1)} %copy-done.1, f32[2320,128]{1,0:T(8,128)S(1)} %collective-permute-done.10.across_in.refs_6_), custom_call_target="tpu_custom_call" | custom-call | flops 8000000 | tf_op jit(solution)/shard_map/pallas_call | solution.py:496
  88.3 14.0 %shard_map.123.near = f32[2048,128]{1,0:T(8,128)S(1)} custom-call(s32[1]{0:T(128)} %bitcast.device.refs_0_, s32[640]{0:T(1024)S(1)} %copy-done.4, f32[2320,128]{1,0:T(8,128)S(1)} %copy-done.1, f32[2320,128]{1,0:T(8,128)S(1)} %collective-permute-done.11.refs_3_, f32[2320,128]{1,0:T(8,128)S(1)} %collective-permute-done.12.refs_4_, ...), custom_call_target="tpu_custom_call" | custom-call | flops 8000000 | tf_op jit(solution)/shard_map/pallas_call | solution.py:529
  102.3 2.9 %shard_map.124 = f32[32,8192]{1,0:T(8,128)} custom-call(s32[1]{0:T(128)} %bitcast.device.refs_0_, s32[64]{0:T(128)S(1)} %copy-done.7, s32[1,27]{1,0:T(1,128)S(1)} %copy-done.8, s32[128]{0:T(128)S(1)} %copy-done.9, f32[32,8,128]{2,1,0:T(8,128)S(1)} %constant_dynamic-update-slice_fusion.piece_0, f32[32,8,128]{2,1,0:T(8,128)S(1)} %collective-permute-done.7.piece_1, ...), custom_call_target="tpu_custom_call" | custom-call | flops 8000000 | tf_op jit(solution)/shard_map/pallas_call | solution.py:546
  (39 shorter events, 0.5 us)
Async XLA Ops:
  6.0 8.1 %collective-permute-start = (f32[2320,128]{1,0:T(8,128)}, f32[2320,128]{1,0:T(8,128)S(1)}, u32[]{:S(2)}, u32[]{:S(2)}) collective-permute-start(f32[2320,128]{1,0:T(8,128)} %get-tuple-element.8.own_in.refs_1_.refs_2_), channel_id=1, source_target_pairs={{0,1},{1,0},{2,3},{3,2},{4,5},{5,4},{6,7},{7,6},{8,9},{9,8},{10,11... | collective-permute-start | bytes 3563528 | tf_op jit(solution)/shard_map/ppermute | solution.py:404
  6.1 82.1 %collective-permute-start.12 = (f32[2320,128]{1,0:T(8,128)}, f32[2320,128]{1,0:T(8,128)S(1)}, u32[]{:S(2)}, u32[]{:S(2)}) collective-permute-start(f32[2320,128]{1,0:T(8,128)} %get-tuple-element.8.own_in.refs_1_.refs_2_), channel_id=1, source_target_pairs={{16,32},{32,16},{17,33},{33,17},{18,34},{34,18},{19,35},{35,19},{2... | collective-permute-start | bytes 3563528 | tf_op jit(solution)/shard_map/ppermute | solution.py:404
  11.3 77.0 %collective-permute-start.11 = (f32[2320,128]{1,0:T(8,128)}, f32[2320,128]{1,0:T(8,128)S(1)}, u32[]{:S(2)}, u32[]{:S(2)}) collective-permute-start(f32[2320,128]{1,0:T(8,128)} %get-tuple-element.8.own_in.refs_1_.refs_2_), channel_id=1, source_target_pairs={{0,16},{16,0},{1,17},{17,1},{2,18},{18,2},{3,19},{19,3},{4,20},{20... | collective-permute-start | bytes 3563528 | tf_op jit(solution)/shard_map/ppermute | solution.py:404
  11.4 50.3 %collective-permute-start.10 = (f32[2320,128]{1,0:T(8,128)}, f32[2320,128]{1,0:T(8,128)S(1)}, u32[]{:S(2)}, u32[]{:S(2)}) collective-permute-start(f32[2320,128]{1,0:T(8,128)} %get-tuple-element.8.own_in.refs_1_.refs_2_), channel_id=1, source_target_pairs={{1,2},{2,1},{3,4},{4,3},{5,6},{6,5},{7,8},{8,7},{9,10},{10,9},{11,... | collective-permute-start | bytes 3563528 | tf_op jit(solution)/shard_map/ppermute | solution.py:404
  14.8 13.4 %collective-permute-start.1 = (f32[1,8,128]{2,1,0:T(8,128)S(1)}, f32[1,8,128]{2,1,0:T(8,128)S(1)}, u32[]{:S(2)}, u32[]{:S(2)}) collective-permute-start(f32[1,8,128]{2,1,0:T(8,128)S(1)} %get-tuple-element.12), channel_id=1, source_target_pairs={{0,2},{2,0},{4,6},{6,4},{8,10},{10,8},{12,14},{14,12},{16,18},{18,... | collective-permute-start | bytes 12296 | tf_op jit(solution)/shard_map/ppermute | solution.py:408
  28.3 4.5 %collective-permute-start.2 = (f32[2,8,128]{2,1,0:T(8,128)S(1)}, f32[2,8,128]{2,1,0:T(8,128)S(1)}, u32[]{:S(2)}, u32[]{:S(2)}) collective-permute-start(f32[2,8,128]{2,1,0:T(8,128)S(1)} %pad_maximum_fusion.2), channel_id=1, source_target_pairs={{0,4},{2,6},{4,0},{6,2},{8,12},{10,14},{12,8},{14,10},{16,20},{18,... | collective-permute-start | bytes 24584 | tf_op jit(solution)/shard_map/ppermute | solution.py:408
  32.8 7.6 %collective-permute-start.3 = (f32[4,8,128]{2,1,0:T(8,128)S(1)}, f32[4,8,128]{2,1,0:T(8,128)S(1)}, u32[]{:S(2)}, u32[]{:S(2)}) collective-permute-start(f32[4,8,128]{2,1,0:T(8,128)S(1)} %pad_maximum_fusion.1), channel_id=1, source_target_pairs={{0,8},{2,10},{4,12},{6,14},{8,0},{10,2},{12,4},{14,6},{16,24},{18,... | collective-permute-start | bytes 49160 | tf_op jit(solution)/shard_map/ppermute | solution.py:408
  40.5 18.5 %collective-permute-start.6 = (f32[8,8,128]{2,1,0:T(8,128)S(1)}, f32[8,8,128]{2,1,0:T(8,128)S(1)}, u32[]{:S(2)}, u32[]{:S(2)}) collective-permute-start(f32[8,8,128]{2,1,0:T(8,128)S(1)} %pad_maximum_fusion), channel_id=1, source_target_pairs={{0,48},{2,50},{4,52},{6,54},{8,56},{10,58},{12,60},{14,62},{16,32}... | collective-permute-start | bytes 98312 | tf_op jit(solution)/shard_map/ppermute | solution.py:408
  41.1 12.4 %collective-permute-start.4 = (f32[8,8,128]{2,1,0:T(8,128)S(1)}, f32[8,8,128]{2,1,0:T(8,128)S(1)}, u32[]{:S(2)}, u32[]{:S(2)}) collective-permute-start(f32[8,8,128]{2,1,0:T(8,128)S(1)} %pad_maximum_fusion), channel_id=1, source_target_pairs={{0,16},{2,18},{4,20},{6,22},{8,24},{10,26},{12,28},{14,30},{16,0},... | collective-permute-start | bytes 98312 | tf_op jit(solution)/shard_map/ppermute | solution.py:408
  53.5 5.4 %collective-permute-start.5 = (f32[8,8,128]{2,1,0:T(8,128)S(1)}, f32[8,8,128]{2,1,0:T(8,128)S(1)}, u32[]{:S(2)}, u32[]{:S(2)}) collective-permute-start(f32[8,8,128]{2,1,0:T(8,128)S(1)} %pad_maximum_fusion), channel_id=1, source_target_pairs={{0,32},{2,34},{4,36},{6,38},{8,40},{10,42},{12,44},{14,46},{16,48}... | collective-permute-start | bytes 98312 | tf_op jit(solution)/shard_map/ppermute | solution.py:408
  59.0 43.3 %collective-permute-start.9 = (f32[32,8,128]{2,1,0:T(8,128)S(1)}, f32[32,8,128]{2,1,0:T(8,128)S(1)}, u32[]{:S(2)}, u32[]{:S(2)}) collective-permute-start(f32[32,8,128]{2,1,0:T(8,128)S(1)} %constant_dynamic-update-slice_fusion.piece_0), channel_id=1, source_target_pairs={{0,192},{2,194},{4,196},{6,198},{8,200},{10,202},{12,204},{14,206}... | collective-permute-start | bytes 393224 | tf_op jit(solution)/shard_map/ppermute | solution.py:408
  59.1 43.2 %collective-permute-start.8 = (f32[32,8,128]{2,1,0:T(8,128)S(1)}, f32[32,8,128]{2,1,0:T(8,128)S(1)}, u32[]{:S(2)}, u32[]{:S(2)}) collective-permute-start(f32[32,8,128]{2,1,0:T(8,128)S(1)} %constant_dynamic-update-slice_fusion.piece_0), channel_id=1, source_target_pairs={{0,128},{2,130},{4,132},{6,134},{8,136},{10,138},{12,140},{14,142}... | collective-permute-start | bytes 393224 | tf_op jit(solution)/shard_map/ppermute | solution.py:408
  61.7 40.6 %collective-permute-start.7 = (f32[32,8,128]{2,1,0:T(8,128)S(1)}, f32[32,8,128]{2,1,0:T(8,128)S(1)}, u32[]{:S(2)}, u32[]{:S(2)}) collective-permute-start(f32[32,8,128]{2,1,0:T(8,128)S(1)} %constant_dynamic-update-slice_fusion.piece_0), channel_id=1, source_target_pairs={{0,64},{2,66},{4,68},{6,70},{8,72},{10,74},{12,76},{14,78},{16,80}... | collective-permute-start | bytes 393224 | tf_op jit(solution)/shard_map/ppermute | solution.py:408
  63.1 1.3 %copy-start = (f32[2320,128]{1,0:T(8,128)S(1)}, f32[2320,128]{1,0:T(8,128)}, u32[]{:S(2)}) copy-start(f32[2320,128]{1,0:T(8,128)} %get-tuple-element.8.own_in.refs_1_.refs_2_) | copy-start | bytes 3563524
  64.4 0.7 copy-start.4
  78.7 6.0 %copy-start.1 = (f32[2320,128]{1,0:T(8,128)S(1)}, f32[2320,128]{1,0:T(8,128)}, u32[]{:S(2)}) copy-start(f32[2320,128]{1,0:T(8,128)} %get-tuple-element.8.own_in.refs_1_.refs_2_) | copy-start | bytes 3563524
  78.7 6.0 %copy-start.6 = (s32[16,27]{1,0:T(8,128)S(1)}, s32[16,27]{1,0:T(8,128)}, u32[]{:S(2)}) copy-start(s32[16,27]{1,0:T(8,128)} %far_in.1) | copy-start | bytes 5188
  88.2 14.1 %copy-start.2 = (f32[2048,128]{1,0:T(8,128)S(1)}, f32[2048,128]{1,0:T(8,128)}, u32[]{:S(2)}) copy-start(f32[2048,128]{1,0:T(8,128)} %get-tuple-element.9.weights) | copy-start | bytes 3145732
  88.2 14.1 %copy-start.3 = (f32[16,32,32]{2,1,0:T(8,128)S(1)}, f32[16,32,32]{2,1,0:T(8,128)}, u32[]{:S(2)}) copy-start(f32[16,32,32]{2,1,0:T(8,128)} %top.1) | copy-start | bytes 196612
  88.2 14.1 %copy-start.5 = (f32[128,2,32]{0,2,1:T(8,128)S(1)}, f32[128,2,32]{0,2,1:T(8,128)}, u32[]{:S(2)}) copy-start(f32[128,2,32]{0,2,1:T(8,128)} %param.19) | copy-start | bytes 98308
  88.2 14.1 %copy-start.7 = (s32[64]{0:T(128)S(1)}, s32[64]{0:T(128)}, u32[]{:S(2)}) copy-start(s32[64]{0:T(128)} %order_in.3) | copy-start | bytes 772
  88.2 14.1 %copy-start.8 = (s32[1,27]{1,0:T(1,128)S(1)}, s32[1,27]{1,0:T(1,128)}, u32[]{:S(2)}) copy-start(s32[1,27]{1,0:T(1,128)} %list_in.1) | copy-start | bytes 328
  88.2 14.1 %copy-start.9 = (s32[128]{0:T(128)S(1)}, s32[128]{0:T(128)}, u32[]{:S(2)}) copy-start(s32[128]{0:T(128)} %map_in.1) | copy-start | bytes 1540
